TPU v7x, 16 devices: a whole 2x2x2 slice. The times are simulated.
16 devices in a mesh: depth: 2 (over z), col: 2 (over y), row: 4 (over x, core).
Axes of the slice: x: 2, y: 2, z: 2, core: 2. Of those that a mesh axis runs over, the one named last changes fastest.
Arguments:
- weight: bfloat16 [2048, 2048], P(('row', 'depth'), 'col')
- rhs_stack: bfloat16 [3, 2048, 8192], P(None, ('row', 'depth'), 'col')
Outputs:
- output: bfloat16 [3, 2048, 8192], P(None, ('row', 'depth'), 'col')
All inputs are finite; a program needn't handle non-finite values.
Results may differ from a plain program's by a relative error of at most 0.001.
Values are sent between devices in bfloat16 or wider.
A program may use at most 1 GiB of HBM per device.

v0:
```python
import jax
import jax.numpy as jnp
from jax import lax
from jax.sharding import PartitionSpec as P

ALL_AXES = ("depth", "col", "row")


def solution(mesh):
    depth_size = mesh.shape["depth"]
    col_size = mesh.shape["col"]
    row_size = mesh.shape["row"]
    group_size = row_size // col_size
    layer_steps = row_size // depth_size
    all_coords = [(layer_idx, col_idx, row_idx) for layer_idx in range(depth_size) for col_idx in range(col_size) for row_idx in range(row_size)]

    def linear_index(coords):
        layer_idx, col_idx, row_idx = coords
        return (layer_idx * col_size + col_idx) * row_size + row_idx

    def a_source(coords, extra):
        layer_idx, col_idx, row_idx = coords
        block_shift = (row_idx + layer_idx * layer_steps) // group_size
        return linear_index((layer_idx, (col_idx + block_shift + extra) % col_size, row_idx))

    def x_source(coords, piece_idx):
        layer_idx, col_idx, row_idx = coords
        src_row = (row_idx + col_idx * group_size + piece_idx + layer_idx * layer_steps) % row_size
        return linear_index((layer_idx, col_idx, src_row))

    perm_a_near = [(a_source(coords, 0), linear_index(coords)) for coords in all_coords]
    perm_a_next = [(a_source(coords, 1), linear_index(coords)) for coords in all_coords]
    perm_x_pieces = [[(x_source(coords, piece_idx), linear_index(coords)) for coords in all_coords] for piece_idx in range(group_size)]
    perm_col_shift = [(col_idx, (col_idx - 1) % col_size) for col_idx in range(col_size)]
    perm_row_shift = [(row_idx, (row_idx - 1) % row_size) for row_idx in range(row_size)]

    def local_product(w_local, x_local):
        rhs_count = x_local.shape[0]
        slice_rows = x_local.shape[1]
        block_cols = x_local.shape[2] // group_size
        w_layer = lax.all_gather(w_local, "depth", axis=0, tiled=True)
        block_rows = w_layer.shape[0]
        x_split = jnp.transpose(x_local.reshape(rhs_count, slice_rows, group_size, block_cols), (2, 1, 0, 3))
        x_layer = lax.all_gather(x_split, "depth", axis=1, tiled=True)
        layer_idx = lax.axis_index("depth")
        row_idx = lax.axis_index("row")
        offset = (row_idx + layer_idx * layer_steps) % group_size
        w_near = lax.ppermute(w_layer, ALL_AXES, perm_a_near)
        if group_size > 1:
            w_next = lax.ppermute(w_layer, ALL_AXES, perm_a_next)
            w_pair = jnp.concatenate([w_near, w_next], axis=1).reshape(block_rows, 2 * group_size, block_rows)
            w_start = lax.dynamic_slice_in_dim(w_pair, offset, group_size, axis=1)
        else:
            w_start = w_near.reshape(block_rows, 1, block_rows)
        w_blocks = jnp.transpose(w_start, (1, 0, 2))
        x_blocks = jnp.stack([lax.ppermute(x_layer[piece_idx], ALL_AXES, perm_x_pieces[piece_idx]) for piece_idx in range(group_size)], axis=0)
        partial_sum = jnp.einsum("tik,tkrm->tirm", w_blocks, x_blocks, preferred_element_type=jnp.float32)
        for step_idx in range(1, layer_steps):
            w_recv = lax.ppermute(w_blocks[0], "col", perm_col_shift)
            w_blocks = jnp.concatenate([w_blocks[1:], w_recv[None]], axis=0)
            x_blocks = lax.ppermute(x_blocks, "row", perm_row_shift)
            partial_sum = partial_sum + jnp.einsum("tik,tkrm->tirm", w_blocks, x_blocks, preferred_element_type=jnp.float32)
        reduced = lax.psum_scatter(partial_sum, "depth", scatter_dimension=1, tiled=True)
        rounded = reduced.astype(jnp.bfloat16)
        return jnp.transpose(rounded, (2, 1, 0, 3)).reshape(rhs_count, slice_rows, group_size * block_cols)

    return jax.shard_map(local_product, mesh=mesh, in_specs=(P(("row", "depth"), "col"), P(None, ("row", "depth"), "col")), out_specs=P(None, ("row", "depth"), "col"), check_vma=False)
```

profile of v0, /device:TPU:0, one launch (start us, length us, event | category | flops | bytes accessed | tf_op | source)
XLA Modules:
  0.0 880.9 jit_solution(11983890257186430565)
XLA Ops:
  6.5 0.0 all-gather.5.cloned.1.call-start
  6.5 8.6 copy.5
  15.1 8.7 copy.6
  23.8 0.0 all-gather.5.cloned.1.call-update
  23.9 0.0 all-gather.3.cloned.1.call-start
  23.9 154.4 %all-gather.5.cloned.1.call-done = bf16[2,512,3,2048]{3,1,2,0:T(8,128)(2,1)} async-done(((bf16[2,256,3,2048]{3,1,2,0:T(8,128)(2,1)}), bf16[2,512,3,2048]{3,1,2,0:T(8,128)(2,1)}) %all-gather.5.cloned.1.call-update) | async-done | bytes 12582928 | tf_op jit(solution)/shard_map/all_gather | solution.py:44
  178.3 5.3 slice_bitcast_fusion.1
  183.6 1.1 collective-permute-start.2
  184.7 0.7 collective-permute-start.3
  185.4 0.0 collective-permute-done.2
  185.4 0.0 copy-start
  185.4 68.5 %collective-permute-done.3 = bf16[512,3,2048]{2,0,1:T(8,128)(2,1)S(1)} collective-permute-done((bf16[512,3,2048]{2,0,1:T(8,128)(2,1)S(1)}, bf16[512,3,2048]{2,0,1:T(8,128)(2,1)S(1)}, u32[]{:S(2)}, u32[]{:S(2)}) %collective-permute-start.3) | collective-permute-done | bytes 6291488 | tf_op jit(solution)/shard_map/ppermute | solution.py:56
  253.9 0.0 copy-start.1
  253.9 0.0 copy-start.2
  253.9 5.3 pad_maximum_fusion
  259.2 0.0 copy-done
  259.2 1.2 copy-done.1
  260.4 1.9 collective-permute-start.5
  262.3 0.0 copy-done.2
  262.3 1.0 copy.3
  263.3 0.0 all-gather.3.cloned.1.call-update
  263.3 0.0 reduce-scatter.2.cloned.1.call-start
  263.4 153.5 %all-gather.3.cloned.1.call-done = bf16[512,1024]{0,1:T(8,128)(2,1)} async-done(((bf16[256,1024]{0,1:T(8,128)(2,1)}), bf16[512,1024]{0,1:T(8,128)(2,1)}) %all-gather.3.cloned.1.call-update) | async-done | bytes 1048592 | tf_op jit(solution)/shard_map/all_gather | solution.py:41
  416.9 3.4 collective-permute-start.1
  420.3 1.9 collective-permute-start
  422.1 21.3 %collective-permute-done.1 = bf16[512,1024]{0,1:T(8,128)(2,1)S(1)} collective-permute-done((bf16[512,1024]{0,1:T(8,128)(2,1)}, bf16[512,1024]{0,1:T(8,128)(2,1)S(1)}, u32[]{:S(2)}, u32[]{:S(2)}) %collective-permute-start.1) | collective-permute-done | bytes 1048608 | tf_op jit(solution)/shard_map/ppermute | solution.py:50
  443.4 0.0 collective-permute-done
  443.4 0.1 pad_maximum_fusion.1
  443.6 0.1 constant_dynamic-slice_fusion
  443.7 0.5 copy.11
  444.2 0.0 slice-start
  444.2 0.1 fusion.5
  444.3 1.5 collective-permute-start.4
  445.8 11.1 %collective-permute-done.4 = bf16[512,512]{1,0:T(8,128)(2,1)S(1)} collective-permute-done((bf16[512,512]{1,0:T(8,128)(2,1)S(1)}, bf16[512,512]{1,0:T(8,128)(2,1)S(1)}, u32[]{:S(2)}, u32[]{:S(2)}) %collective-permute-start.4) | collective-permute-done | bytes 524320 | tf_op jit(solution)/shard_map/ppermute | solution.py:59
  456.9 0.0 collective-permute-done.5
  456.9 0.0 slice-start.1
  456.9 16.4 %fusion = f32[2,512,3,2048]{3,1,2,0:T(8,128)} fusion(bf16[2,512,3,2048]{3,1,2,0:T(8,128)(2,1)} %collective-permute-done.5, bf16[1,512,512]{2,1,0:T(8,128)(2,1)S(1)} %bitcast.39, bf16[1,512,512]{2,1,0:T(8,128)(2,1)S(1)} %get-tuple-element.7), kind=kOutput, calls=%fused_computation.7 | convolution fusion | flops 6444548096 | bytes 38797312 | tf_op jit(solution)/shard_map/tik,tkrm->tirm/dot_general | solution.py:62
  473.3 0.0 slice-done
  473.3 0.0 slice-done.1
  473.3 22.0 %convolution_add_fusion = f32[2,512,3,2048]{3,1,2,0:T(8,128)} fusion(f32[2,512,3,2048]{3,1,2,0:T(8,128)} %fusion, bf16[512,2,512]{2,0,1:T(8,128)(2,1)S(1)} %copy.11, bf16[1,512,3,2048]{3,1,2,0:T(8,128)(2,1)} %bitcast.36, bf16[1,512,3,2048]{3,1,2,0:T(8,128)(2,1)S(1)} %bitcast.34), kind=kOutput, calls=%fused_computation.1 | convolution fusion | flops 6473908224 | bytes 63963136 | tf_op jit(solution)/shard_map/tik,tkrm->tirm/dot_general | solution.py:57
  495.4 0.0 reduce-scatter.2.cloned.1.call-update
  495.4 353.5 %reduce-scatter.2.cloned.1.call-done = f32[2,256,3,2048]{3,1,2,0:T(8,128)} async-done(((f32[2,512,3,2048]{3,1,2,0:T(8,128)}), f32[2,256,3,2048]{3,1,2,0:T(8,128)}) %reduce-scatter.2.cloned.1.call-update) | async-done | bytes 12582928 | tf_op jit(solution)/shard_map/reduce_scatter | solution.py:63
  848.9 8.3 convert_bitcast_fusion
  857.2 8.6 copy.7
  865.7 8.6 copy.8
  (1 shorter events, 0.0 us)
Async XLA Ops:
  6.5 171.8 %all-gather.5.cloned.1.call-start = ((), (), s32[]{:S(2)}) async-start(), calls=%async_computation.2 | async-start | bytes 18874368 | tf_op jit(solution)/shard_map/all_gather | solution.py:44
  23.9 393.0 %all-gather.3.cloned.1.call-start = ((), (), s32[]{:S(2)}) async-start(), calls=%async_computation.1 | async-start | bytes 1572864 | tf_op jit(solution)/shard_map/all_gather | solution.py:41
  183.6 1.8 collective-permute-start.2
  184.7 69.2 %collective-permute-start.3 = (bf16[512,3,2048]{2,0,1:T(8,128)(2,1)S(1)}, bf16[512,3,2048]{2,0,1:T(8,128)(2,1)S(1)}, u32[]{:S(2)}, u32[]{:S(2)}) collective-permute-start(bf16[512,3,2048]{2,0,1:T(8,128)(2,1)S(1)} %get-tuple-element.6), channel_id=1, source_target_pairs={{1,0},{2,1},{3,2},{0,3},{7,4},{4,5},{5,6},{6,7},{11,8},{8,9},{9,10... | collective-permute-start | bytes 18874376 | tf_op jit(solution)/shard_map/ppermute | solution.py:56
  185.4 73.8 %copy-start = (bf16[512,3,2048]{2,0,1:T(8,128)(2,1)}, bf16[512,3,2048]{2,0,1:T(8,128)(2,1)S(1)}, u32[]{:S(2)}) copy-start(bf16[512,3,2048]{2,0,1:T(8,128)(2,1)S(1)} %collective-permute-done.2) | copy-start | bytes 18874372
  253.9 6.5 copy-start.1
  253.9 8.4 copy-start.2
  260.4 196.5 %collective-permute-start.5 = (bf16[2,512,3,2048]{3,1,2,0:T(8,128)(2,1)}, bf16[2,512,3,2048]{3,1,2,0:T(8,128)(2,1)}, u32[]{:S(2)}, u32[]{:S(2)}) collective-permute-start(bf16[2,512,3,2048]{3,1,2,0:T(8,128)(2,1)} %pad_maximum_fusion), channel_id=1, source_target_pairs={{0,3},{1,0},{2,1},{3,2},{4,7},{5,4},{6,5},{7,6},{8,11},{9,8},{10,9... | collective-permute-start | bytes 37748744 | tf_op jit(solution)/shard_map/ppermute | solution.py:61
  263.3 585.6 %reduce-scatter.2.cloned.1.call-start = ((), (), s32[]{:S(2)}) async-start(), calls=%async_computation.3 | async-start | bytes 37748736 | tf_op jit(solution)/shard_map/reduce_scatter | solution.py:63
  416.9 26.5 %collective-permute-start.1 = (bf16[512,1024]{0,1:T(8,128)(2,1)}, bf16[512,1024]{0,1:T(8,128)(2,1)S(1)}, u32[]{:S(2)}, u32[]{:S(2)}) collective-permute-start(bf16[512,1024]{0,1:T(8,128)(2,1)} %all-gather.3.cloned.1.call-done), channel_id=1, source_target_pairs={{4,0},{5,1},{2,2},{3,3},{0,4},{1,5},{6,6},{7,7},{8,8},{9,9},{14,10... | collective-permute-start | bytes 3145736 | tf_op jit(solution)/shard_map/ppermute | solution.py:50
  420.3 23.2 %collective-permute-start = (bf16[512,1024]{0,1:T(8,128)(2,1)}, bf16[512,1024]{0,1:T(8,128)(2,1)S(1)}, u32[]{:S(2)}, u32[]{:S(2)}) collective-permute-start(bf16[512,1024]{0,1:T(8,128)(2,1)} %all-gather.3.cloned.1.call-done), channel_id=1, source_target_pairs={{0,0},{1,1},{6,2},{7,3},{4,4},{5,5},{2,6},{3,7},{12,8},{13,9},{10,... | collective-permute-start | bytes 3145736 | tf_op jit(solution)/shard_map/ppermute | solution.py:48
  444.2 29.1 %slice-start = ((s8[6291456]{0:T(1024)(128)(4,1)}), s8[4194304]{0:T(1024)(128)(4,1)S(1)}, s32[]{:S(2)}) async-start(s8[6291456]{0:T(1024)(128)(4,1)} %bitcast.32), calls=%async_computation.4 | async-start | bytes 8388608
  444.3 12.6 %collective-permute-start.4 = (bf16[512,512]{1,0:T(8,128)(2,1)S(1)}, bf16[512,512]{1,0:T(8,128)(2,1)S(1)}, u32[]{:S(2)}, u32[]{:S(2)}) collective-permute-start(bf16[512,512]{1,0:T(8,128)(2,1)S(1)} %get-tuple-element.8), channel_id=1, source_target_pairs={{0,4},{4,0},{1,5},{5,1},{2,6},{6,2},{3,7},{7,3},{8,12},{12,8},{9,1... | collective-permute-start | bytes 1572872 | tf_op jit(solution)/shard_map/ppermute | solution.py:59
  456.9 16.4 %slice-start.1 = ((s8[6291456]{0:T(1024)(128)(4,1)}), s8[2097152]{0:T(1024)(128)(4,1)S(1)}, s32[]{:S(2)}) async-start(s8[6291456]{0:T(1024)(128)(4,1)} %bitcast.32), calls=%async_computation.5 | async-start | bytes 4194304
Sparse Core Ops, SparseCore 0:
  24.0 154.2 all-gather.4
  263.4 153.4 all-gather.2
  495.5 353.3 reduce-scatter.1
where the time goes:
time: 882 us; the launch traced here: 881 us
  waiting for transfers between devices  762 us (86%)
  local copies, waits for them, and re-layouts  42.7 us (5%)
  matrix products  38.5 us (4%)
  other arithmetic  13.7 us (2%)
  between operations  13.2 us (1%)
  starting transfers between devices  10.5 us (1%)
    reduce_scatter x1, waiting for transfers between devices, local_product(): lax.psum_scatter(partial_sum, 'depth', scatter_dimension=1, tiled=True)  353 us
    all_gather x1, waiting for transfers between devices, local_product(): x_layer = lax.all_gather(x_split, 'depth', axis=1, tiled=True)  154 us
    all_gather x1, waiting for transfers between devices, local_product(): w_layer = lax.all_gather(w_local, 'depth', axis=0, tiled=True)  154 us
    ppermute x2, waiting for transfers between devices, local_product(): lax.ppermute(x_layer[piece_idx], ALL_AXES, perm_x_pieces[piece_idx])  68.5 us
    dot_general x2, matrix products, local_product(): jnp.einsum('tik,tkrm->tirm', w_blocks, x_blocks, preferred_element_type=j...  38.5 us
    ppermute x1, waiting for transfers between devices, local_product(): w_next = lax.ppermute(w_layer, ALL_AXES, perm_a_next)  21.3 us
  transfers between devices with their start and end apart: 9, of which 6 were waited for; matrix products, arithmetic and copies ran while one was open for 0% of the time, Pallas kernels for 0%

commit v1 on v0

v1 whole, which is shorter than its diff:
```python
import jax
import jax.numpy as jnp
from jax import lax
from jax.sharding import PartitionSpec as P


def solution(mesh):
    plane = ("row", "depth")

    def local(w, x):
        w = lax.all_gather(w, "col", axis=1, tiled=True)
        w = lax.all_gather(w, plane, axis=0, tiled=True)
        xs = lax.all_to_all(x, plane, split_axis=2, concat_axis=1, tiled=True)
        y = jnp.einsum("mk,rkn->rmn", w, xs, preferred_element_type=jnp.float32).astype(jnp.bfloat16)
        return lax.all_to_all(y, plane, split_axis=1, concat_axis=2, tiled=True)

    return jax.shard_map(local, mesh=mesh, in_specs=(P(("row", "depth"), "col"), P(None, ("row", "depth"), "col")),
                         out_specs=P(None, ("row", "depth"), "col"), check_vma=False)
```

time: 882 us -> 338 us (0.38)
  waiting for transfers between devices: 762 us -> 24.3 us
  blocking collectives: 0 us -> 218 us
  local copies, waits for them, and re-layouts: 42.7 us -> 62.6 us
  matrix products: 38.5 us -> 18.9 us
  other arithmetic: 13.7 us -> 0 us
  starting transfers between devices: 10.5 us -> 0.04 us
    reduce_scatter x1 -> x0, waiting for transfers between devices: 353 us -> none  [local_product(): lax.psum_scatter(partial_sum, 'depth', scatter_dimension=1, tiled=True)]
    all_gather x2, waiting for transfers between devices: 308 us -> 23.6 us  [the longest x1 23.6 us: local(): w = lax.all_gather(w, 'col', axis=1, tiled=True)]
    all_to_all x0 -> x2, blocking collectives: none -> 218 us  [the longest x1 121 us: local(): xs = lax.all_to_all(x, plane, split_axis=2, concat_axis=1, tiled=True)]
    ppermute x6 -> x0, waiting for transfers between devices: 101 us -> none  [the longest x2 68.5 us: local_product(): lax.ppermute(x_layer[piece_idx], ALL_AXES, perm_x_pieces[piece_idx])]
    all_to_all x0 -> x4, local copies, waits for them, and re-layouts: none -> 35.5 us  [the longest x2 17.8 us: local(): xs = lax.all_to_all(x, plane, split_axis=2, concat_axis=1, tiled=True)]
    dot_general x2 -> x1, matrix products: 38.5 us -> 18.9 us  [local(): jnp.einsum('mk,rkn->rmn', w, xs, preferred_element_type=jnp.float32)]
    reshape x2 -> x0, local copies, waits for them, and re-layouts: 17.3 us -> none  [the longest x1 8.69 us: local_product(): x_local.reshape(rhs_count, slice_rows, group_size, block_cols)]
    convert_element_type x0 -> x1, local copies, waits for them, and re-layouts: none -> 14.1 us  [local(): jnp.einsum('mk,rkn->rmn', w, xs, preferred_element_type=jnp.float32)]
  transfers between devices with their start and end apart: 9 -> 2, of which waited for: 6 -> 1; matrix products, arithmetic and copies ran while one was open for 0% -> 6% of each run, Pallas kernels for 0% -> 0%
where the time goes in v1:
time: 338 us; the launch traced here: 337 us
  blocking collectives  218 us (64%)
  local copies, waits for them, and re-layouts  62.6 us (19%)
  waiting for transfers between devices  24.3 us (7%)
  matrix products  18.9 us (6%)
  between operations  13.4 us (4%)
    all_to_all x1, blocking collectives, local(): xs = lax.all_to_all(x, plane, split_axis=2, concat_axis=1, tiled=True)  121 us
    all_to_all x1, blocking collectives, local(): return lax.all_to_all(y, plane, split_axis=1, concat_axis=2, tiled=True)  96.7 us
    all_gather x1, waiting for transfers between devices, local(): w = lax.all_gather(w, 'col', axis=1, tiled=True)  23.6 us
    dot_general x1, matrix products, local(): jnp.einsum('mk,rkn->rmn', w, xs, preferred_element_type=jnp.float32)  18.9 us
    all_to_all x2, local copies, waits for them, and re-layouts, local(): xs = lax.all_to_all(x, plane, split_axis=2, concat_axis=1, tiled=True)  17.8 us
    all_to_all x2, local copies, waits for them, and re-layouts, local(): return lax.all_to_all(y, plane, split_axis=1, concat_axis=2, tiled=True)  17.7 us
    convert_element_type x1, local copies, waits for them, and re-layouts, local(): jnp.einsum('mk,rkn->rmn', w, xs, preferred_element_type=jnp.float32)  14.1 us
    unnamed x1, local copies, waits for them, and re-layouts  13.1 us
  transfers between devices with their start and end apart: 2, of which 1 were waited for; matrix products, arithmetic and copies ran while one was open for 6% of the time, Pallas kernels for 0%

profile of v1, /device:TPU:0, one launch (start us, length us, event | category | flops | bytes accessed | tf_op | source)
XLA Modules:
  0.0 336.9 jit_solution(6897963277432379223)
XLA Ops:
  6.5 0.0 all-gather.3.cloned.1.call-start
  6.5 0.7 all-gather.3.cloned.1.call-update
  7.3 0.0 all-gather.5.cloned.1.call-start
  7.3 23.6 %all-gather.3.cloned.1.call-done = bf16[256,2048]{1,0:T(8,128)(2,1)} async-done(((bf16[256,1024]{1,0:T(8,128)(2,1)}), bf16[256,2048]{1,0:T(8,128)(2,1)}) %all-gather.3.cloned.1.call-update) | async-done | bytes 1048592 | tf_op jit(solution)/shard_map/all_gather | solution.py:11
  30.9 0.0 all-gather.5.cloned.1.call-update
  30.9 13.1 %copy.5 = bf16[3,256,4096]{1,0,2:T(4,128)(2,1)} copy(bf16[3,256,4096]{2,1,0:T(8,128)(2,1)} %param.3) | data formatting | bytes 12582912 | tf_op args[1]
  44.0 120.9 %all_to_all.36 = bf16[3,256,4096]{1,0,2:T(4,128)(2,1)S(1)} all-to-all(bf16[3,256,4096]{1,0,2:T(4,128)(2,1)} %copy.5), channel_id=1, replica_groups=mesh['depth'=2,'col'=2,'row'=4] {'row','depth'}, dimensions={2} | all-to-all | bytes 12582912 | tf_op jit(solution)/shard_map/all_to_all | solution.py:13
  164.9 7.4 %copy.10 = bf16[3,256,8,512]{1,2,3,0:T(8,128)(2,1)} copy(bf16[3,256,8,512]{1,0,3,2:T(4,128)(2,1)S(1)} %bitcast.21) | data formatting | bytes 12582912 | tf_op jit(solution)/shard_map/all_to_all | solution.py:13
  172.3 10.4 %all_to_all.29 = bf16[3,2048,512]{1,2,0:T(8,128)(2,1)} reshape(bf16[3,8,256,512]{2,1,3,0:T(8,128)(2,1)} %bitcast.23) | data formatting | bytes 12582912 | tf_op jit(solution)/shard_map/all_to_all | solution.py:13
  182.7 0.0 all-gather.5.cloned.1.call-done
  182.7 18.9 %convert_bitcast_fusion = bf16[3,2048,512]{1,2,0:T(8,128)(2,1)} fusion(bf16[3,2048,512]{1,2,0:T(8,128)(2,1)} %all_to_all.29, bf16[2048,2048]{1,0:T(8,128)(2,1)} %all-gather.5.cloned.1.call-done), kind=kOutput, calls=%fused_computation.3 | convolution fusion | flops 12888047616 | bytes 20971520 | tf_op jit(solution)/shard_map/mk,rkn->rmn/dot_general | solution.py:14
  201.7 14.1 %copy.7 = bf16[3,2048,512]{2,0,1:T(4,128)(2,1)} copy(bf16[3,2048,512]{1,2,0:T(8,128)(2,1)} %convert_bitcast_fusion) | data formatting | bytes 12582912 | tf_op jit(solution)/shard_map/convert_element_type | solution.py:14
  215.8 96.7 %all_to_all.37 = bf16[3,2048,512]{2,0,1:T(4,128)(2,1)S(1)} all-to-all(bf16[3,2048,512]{2,0,1:T(4,128)(2,1)} %copy.7), channel_id=1, replica_groups=mesh['depth'=2,'col'=2,'row'=4] {'row','depth'}, dimensions={1} | all-to-all | bytes 12582912 | tf_op jit(solution)/shard_map/all_to_all | solution.py:15
  312.4 7.3 %copy.8 = bf16[3,256,8,512]{3,2,1,0:T(8,128)(2,1)} copy(bf16[3,256,8,512]{3,0,1,2:T(4,128)(2,1)S(1)} %bitcast.22) | data formatting | bytes 12582912 | tf_op jit(solution)/shard_map/all_to_all | solution.py:15
  319.7 10.4 %all_to_all.33 = bf16[3,256,4096]{2,1,0:T(8,128)(2,1)} reshape(bf16[3,256,8,512]{3,2,1,0:T(8,128)(2,1)} %copy.8) | data formatting | bytes 12582912 | tf_op jit(solution)/shard_map/all_to_all | solution.py:15
Async XLA Ops:
  6.5 24.3 %all-gather.3.cloned.1.call-start = ((), (), s32[]{:S(2)}) async-start(), calls=%async_computation.2 | async-start | bytes 1572864 | tf_op jit(solution)/shard_map/all_gather | solution.py:11
  7.3 175.5 %all-gather.5.cloned.1.call-start = ((), (), s32[]{:S(2)}) async-start(), calls=%async_computation.3 | async-start | bytes 9437184 | tf_op jit(solution)/shard_map/all_gather | solution.py:12
Sparse Core Ops, SparseCore 0:
  8.9 21.9 all-gather.2
  32.7 103.9 all-gather.4

commit v2 on v1

v2 whole, which is shorter than its diff:
```python
import functools

import jax
import jax.numpy as jnp
from jax import lax
from jax.experimental import pallas as pl
from jax.experimental.pallas import tpu as pltpu
from jax.sharding import PartitionSpec as P

MESH = pl.DeviceIdType.MESH
PEERS = 8
HALVES = 2
PIECE = 256


def kernel(w_ref, x_ref, y_ref, a_buf, x_buf, y_buf, a_send, a_recv, x_send, x_recv, y_send, y_recv, own_sem):
    z, j, row = lax.axis_index("depth"), lax.axis_index("col"), lax.axis_index("row")
    x, c = row // 2, row % 2
    rhs, rows, _ = x_ref.shape
    kcols = w_ref.shape[1]
    chunks = rhs * HALVES

    def place(px, pc, pz):
        return (px * 2 + pc) * 2 + pz

    def peer(k):
        kx, kc, kz = k // 4 % 2, k // 2 % 2, k % 2
        px = x + kx * (1 - 2 * x)
        pc = c + kc * (1 - 2 * c)
        pz = z + kz * (1 - 2 * z)
        return (pz, j, px * 2 + pc), place(px, pc, pz)

    me = place(x, c, z)

    def a_block(g, jj):
        return a_buf.at[pl.ds(pl.multiple_of(g * rows, rows), rows), pl.ds(pl.multiple_of(jj * kcols, kcols), kcols)]

    fx, fz = x + (1 - c) * (1 - 2 * x), z + c * (1 - 2 * z)
    sx, sz = x + c * (1 - 2 * x), z + (1 - c) * (1 - 2 * z)
    first, second = (fz, j, fx * 2 + c), (sz, j, sx * 2 + c)
    other_y, other_core = (z, 1 - j, row), (z, j, x * 2 + 1 - c)
    spots = [(x, z), (fx, fz), (sx, sz), (1 - x, 1 - z)]
    mine = [place(px, c, pz) for px, pz in spots]
    theirs = [place(px, 1 - c, pz) for px, pz in (spots[0], spots[2], spots[1], spots[3])]

    def a_copy(n):
        if n == 0:
            src, here, there, to = w_ref, a_block(mine[1], j), a_block(me, j), first
        elif n == 1:
            src, here, there, to = w_ref, a_block(mine[2], j), a_block(me, j), second
        elif n == 2:
            src, here, there, to = a_block(mine[1], j), a_block(mine[3], j), a_block(mine[1], j), second
        elif n < 7:
            b = n - 3
            there = a_block(mine[b], j)
            src, here, to = (w_ref if b == 0 else there), a_block(mine[b], 1 - j), other_y
        elif n < 11:
            b = n - 7
            there = a_block(mine[b], j)
            src, here, to = (w_ref if b == 0 else there), a_block(theirs[b], j), other_core
        else:
            b = n - 11
            there = a_block(mine[b], 1 - j)
            src, here, to = there, a_block(theirs[b], 1 - j), other_core
        send = pltpu.make_async_remote_copy(src, there, a_send.at[n], a_recv.at[n], device_id=to, device_id_type=MESH)
        recv = pltpu.make_async_remote_copy(src, here, a_send.at[n], a_recv.at[n], device_id=to, device_id_type=MESH)
        return send, recv

    def a_start(n):
        a_copy(n)[0].start()

    def a_wait(n):
        a_copy(n)[1].wait_recv()

    def x_cols(chunk, g):
        return x_ref.at[chunk // HALVES, :, pl.ds(pl.multiple_of(g * (HALVES * PIECE) + chunk % HALVES * PIECE, PIECE), PIECE)]

    def x_rows(chunk, g):
        return x_buf.at[chunk, pl.ds(pl.multiple_of(g * rows, rows), rows), :]

    def x_copy(chunk, k, receive=False):
        dev, g = peer(k)
        return pltpu.make_async_remote_copy(
            x_cols(chunk, g), x_rows(chunk, g if receive else me), x_send.at[chunk, k], x_recv.at[chunk, k],
            device_id=dev, device_id_type=MESH)

    def y_rows(chunk, g):
        return y_buf.at[chunk, pl.ds(pl.multiple_of(g * rows, rows), rows), :]

    def y_cols(chunk, g):
        return y_ref.at[chunk // HALVES, :, pl.ds(pl.multiple_of(g * (HALVES * PIECE) + chunk % HALVES * PIECE, PIECE), PIECE)]

    def y_copy(chunk, k, receive=False):
        dev, g = peer(k)
        return pltpu.make_async_remote_copy(
            y_rows(chunk, g), y_cols(chunk, g if receive else me), y_send.at[chunk, k], y_recv.at[chunk, k],
            device_id=dev, device_id_type=MESH)

    def own_x(chunk):
        return pltpu.make_async_copy(x_cols(chunk, me), x_rows(chunk, me), own_sem.at[chunk])

    def own_y(chunk):
        return pltpu.make_async_copy(y_rows(chunk, me), y_cols(chunk, me), own_sem.at[chunks + 1 + chunk])

    own_a = pltpu.make_async_copy(w_ref, a_block(me, j), own_sem.at[chunks])

    def send_x(chunk):
        own_x(chunk).start()
        for k in (5, 4, 1, 7, 6, 3, 2):
            x_copy(chunk, k).start()

    barrier = pltpu.get_barrier_semaphore()
    for k in range(1, PEERS):
        pl.semaphore_signal(barrier, inc=1, device_id=peer(k)[0], device_id_type=MESH)
    pl.semaphore_signal(barrier, inc=1, device_id=other_y, device_id_type=MESH)
    pl.semaphore_wait(barrier, PEERS)

    own_a.start()
    for n in (0, 1, 3, 7):
        a_start(n)
    send_x(0)
    a_wait(0)
    for n in (2, 4, 8):
        a_start(n)
    a_wait(1)
    for n in (5, 9):
        a_start(n)
    send_x(1)
    a_wait(2)
    for n in (6, 10):
        a_start(n)
    for chunk in range(2, chunks):
        send_x(chunk)
    for b in range(4):
        a_wait(3 + b)
        a_start(11 + b)
    for n in range(7, 15):
        a_wait(n)
    own_a.wait()

    def do_chunk(chunk, carry):
        own_x(chunk).wait()

        def arrive(k, carry):
            x_copy(chunk, k, receive=True).wait_recv()
            return carry

        lax.fori_loop(1, PEERS, arrive, 0)

        def tile(t, carry):
            k = (t + 1) % PEERS
            g = peer(k)[1]
            at = pl.ds(pl.multiple_of(g * rows, rows), rows)
            acc = jnp.dot(a_buf[at, :], x_buf[chunk], preferred_element_type=jnp.float32)
            y_buf[chunk, at, :] = acc.astype(y_buf.dtype)

            @pl.when(t > 0)
            def _():
                y_copy(chunk, t).start()

            return carry

        lax.fori_loop(0, PEERS, tile, 0)
        return carry

    lax.fori_loop(0, chunks, do_chunk, 0)

    for n in range(15):
        a_copy(n)[0].wait_send()

    def x_done(chunk, carry):
        def one(k, carry):
            x_copy(chunk, k).wait_send()
            return carry

        return lax.fori_loop(1, PEERS, one, carry)

    lax.fori_loop(0, chunks, x_done, 0)

    def own_out(chunk, carry):
        own_y(chunk).start()
        return carry

    lax.fori_loop(0, chunks, own_out, 0)

    def y_done(chunk, carry):
        def one(k, carry):
            y_copy(chunk, k).wait_send()
            y_copy(chunk, k, receive=True).wait_recv()
            return carry

        lax.fori_loop(1, PEERS, one, 0)
        own_y(chunk).wait()
        return carry

    lax.fori_loop(0, chunks, y_done, 0)


def solution(mesh):
    def local(w, x):
        rhs, rows, cols = x.shape
        n = rows * PEERS
        chunks = rhs * HALVES
        return pl.pallas_call(
            kernel,
            out_shape=jax.ShapeDtypeStruct(x.shape, x.dtype),
            in_specs=[pl.BlockSpec(memory_space=pl.ANY)] * 2,
            out_specs=pl.BlockSpec(memory_space=pl.ANY),
            scratch_shapes=[
                pltpu.VMEM((n, n), w.dtype),
                pltpu.VMEM((chunks, n, PIECE), x.dtype),
                pltpu.VMEM((chunks, n, PIECE), x.dtype),
                pltpu.SemaphoreType.DMA((15,)),
                pltpu.SemaphoreType.DMA((15,)),
                pltpu.SemaphoreType.DMA((chunks, PEERS)),
                pltpu.SemaphoreType.DMA((chunks, PEERS)),
                pltpu.SemaphoreType.DMA((chunks, PEERS)),
                pltpu.SemaphoreType.DMA((chunks, PEERS)),
                pltpu.SemaphoreType.DMA((2 * chunks + 1,)),
            ],
            compiler_params=pltpu.CompilerParams(collective_id=0, has_side_effects=True, vmem_limit_bytes=48 * 1024 * 1024),
        )(w, x)

    return jax.shard_map(local, mesh=mesh, in_specs=(P(("row", "depth"), "col"), P(None, ("row", "depth"), "col")),
                         out_specs=P(None, ("row", "depth"), "col"), check_vma=False)
```

time: 338 us -> 168 us (0.50)
  blocking collectives: 218 us -> 0 us
  Pallas kernels: 0 us -> 160 us
  local copies, waits for them, and re-layouts: 62.6 us -> 7.33 us
  waiting for transfers between devices: 24.3 us -> 0 us
  matrix products: 18.9 us -> 0 us
  between operations: 13.4 us -> 0.01 us
    all_to_all x2 -> x0, blocking collectives: 218 us -> none  [the longest x1 121 us: local(): xs = lax.all_to_all(x, plane, split_axis=2, concat_axis=1, tiled=True)]
    pallas_call x0 -> x1, Pallas kernels: none -> 160 us  [local(): pl.pallas_call(kernel, out_shape=jax.ShapeDtypeStruct(x.shape, x.dtype),...]
    all_to_all x4 -> x0, local copies, waits for them, and re-layouts: 35.5 us -> none  [the longest x2 17.8 us: local(): xs = lax.all_to_all(x, plane, split_axis=2, concat_axis=1, tiled=True)]
    all_gather x2 -> x0, waiting for transfers between devices: 23.6 us -> none  [the longest x1 23.6 us: local(): w = lax.all_gather(w, 'col', axis=1, tiled=True)]
    dot_general x1 -> x0, matrix products: 18.9 us -> none  [local(): jnp.einsum('mk,rkn->rmn', w, xs, preferred_element_type=jnp.float32)]
    convert_element_type x1 -> x0, local copies, waits for them, and re-layouts: 14.1 us -> none  [local(): jnp.einsum('mk,rkn->rmn', w, xs, preferred_element_type=jnp.float32)]
    unnamed x1 -> x3, local copies, waits for them, and re-layouts: 13.1 us -> 7.33 us
  transfers between devices with their start and end apart: 2 -> 0, of which waited for: 1 -> 0; matrix products, arithmetic and copies ran while one was open for 6% -> 0% of each run, Pallas kernels for 0% -> 0%
where the time goes in v2:
time: 168 us
  Pallas kernels  160 us (95%)
  local copies, waits for them, and re-layouts  7.33 us (4%)
    pallas_call x1, Pallas kernels, local(): pl.pallas_call(kernel, out_shape=jax.ShapeDtypeStruct(x.shape, x.dtype),...  160 us
    unnamed x3, local copies, waits for them, and re-layouts  7.33 us

profile of v2, /device:TPU:0, one launch (start us, length us, event | category | flops | bytes accessed | tf_op | source)
XLA Modules:
  0.0 167.7 jit_solution(6860187089907690705)
XLA Ops:
  0.0 0.0 copy-start
  0.0 1.0 copy-done
  1.0 160.4 %shard_map.28 = bf16[3,256,4096]{2,1,0:T(8,128)(2,1)} custom-call(bf16[256,1024]{1,0:T(8,128)(2,1)S(1)} %copy-done, bf16[3,256,4096]{2,1,0:T(8,128)(2,1)} %x_ref.1), custom_call_target="tpu_custom_call" | custom-call | tf_op jit(solution)/shard_map/pallas_call | solution.py:204
  161.4 6.3 %copy.4 = bf16[3,256,4096]{2,1,0:T(8,128)(2,1)} copy(bf16[3,256,4096]{2,1,0:T(8,128)(2,1)} %shard_map.28) | data formatting | bytes 12582912
Async XLA Ops:
  0.0 1.0 copy-start

commit v3 on v1

v3 whole, which is shorter than its diff:
```python
import jax
import jax.numpy as jnp
from jax import lax
from jax.experimental import pallas as pl
from jax.experimental.pallas import tpu as pltpu
from jax.sharding import PartitionSpec as P

MESH = pl.DeviceIdType.MESH
SIDE = 4
BLOCKS = 2 * SIDE
PIECE = 256
AHEAD = 3
LAG = 1


def kernel(w_ref, x_ref, y_ref, a_buf, x_buf, y_buf, a_send, a_recv, x_send, x_recv, y_send, y_recv, own_sem):
    z, j, row = lax.axis_index("depth"), lax.axis_index("col"), lax.axis_index("row")
    x, c = row // 2, row % 2
    rhs, rows, cols = x_ref.shape
    kcols = w_ref.shape[1]
    group = cols // SIDE
    pieces = group // PIECE
    steps = rhs * pieces

    def peer(k):
        kx, kc, kz = k // 4 % 2, k // 2 % 2, k % 2
        return x + kx * (1 - 2 * x), c + kc * (1 - 2 * c), z + kz * (1 - 2 * z)

    def device(k):
        px, pc, pz = peer(k)
        return (pz, j, px * 2 + pc)

    def in_side(k):
        _, pc, pz = peer(k)
        return pc * 2 + pz

    def in_plane(k):
        return peer(k)[0] * SIDE + in_side(k)

    other_y = (z, 1 - j, row)

    def a_block(k, jj):
        return a_buf.at[pl.ds(pl.multiple_of(in_side(k) * rows, rows), rows), pl.ds(pl.multiple_of(jj * kcols, kcols), kcols)]

    def a_copy(n, receive=False):
        own = (w_ref, a_block(0, j))
        src, there, here, to = (
            own + (a_block(1, j), device(1)),
            own + (a_block(0, 1 - j), other_y),
            (a_block(1, j),) * 2 + (a_block(1, 1 - j), other_y),
            own + (a_block(2, j), device(2)),
            (a_block(1, j),) * 2 + (a_block(3, j), device(2)),
            (a_block(0, 1 - j),) * 2 + (a_block(2, 1 - j), device(2)),
            (a_block(1, 1 - j),) * 2 + (a_block(3, 1 - j), device(2)),
        )[n]
        return pltpu.make_async_remote_copy(
            src, here if receive else there, a_send.at[n], a_recv.at[n], device_id=to, device_id_type=MESH)

    def columns(step, k):
        at = in_side(k) * group + step % pieces * PIECE
        return (step // pieces, slice(None), pl.ds(pl.multiple_of(at, PIECE), PIECE))

    def x_rows(step, k):
        return x_buf.at[step, pl.ds(pl.multiple_of(in_plane(k) * rows, rows), rows), :]

    def x_copy(step, k, receive=False):
        if k in (5, 7):
            src, there, to = x_rows(step, k - 4), x_rows(step, k - 4), device(4)
        else:
            src, there, to = x_ref.at[columns(step, k)], x_rows(step, 0), device(k)
        return pltpu.make_async_remote_copy(
            src, x_rows(step, k) if receive else there, x_send.at[step, k], x_recv.at[step, k],
            device_id=to, device_id_type=MESH)

    def y_rows(step, k):
        return y_buf.at[step, pl.ds(pl.multiple_of(in_side(k) * rows, rows), rows), :]

    def y_copy(step, k, receive=False):
        return pltpu.make_async_remote_copy(
            y_rows(step, k), y_ref.at[columns(step, k if receive else 0)], y_send.at[step, k], y_recv.at[step, k],
            device_id=device(k), device_id_type=MESH)

    def own_x(step):
        return pltpu.make_async_copy(x_ref.at[columns(step, 0)], x_rows(step, 0), own_sem.at[0, step])

    def own_y(step):
        return pltpu.make_async_copy(y_rows(step, 0), y_ref.at[columns(step, 0)], own_sem.at[1, step])

    own_a = pltpu.make_async_copy(w_ref, a_block(0, j), own_sem.at[2, 0])

    def send_x(step, ks):
        for k in ks:
            x_copy(step, k).start()

    def loop(low, high, body):
        def one(step, carry):
            body(step)
            return carry

        lax.fori_loop(low, high, one, 0)

    barrier = pltpu.get_barrier_semaphore()
    for to in [device(k) for k in (1, 2, 3, 4, 6)] + [other_y]:
        pl.semaphore_signal(barrier, inc=1, device_id=to, device_id_type=MESH)
    pl.semaphore_wait(barrier, 6)

    for n in (0, 1, 3):
        a_copy(n).start()
    own_a.start()

    def first(step):
        send_x(step, (1, 3))

        @pl.when(step < AHEAD)
        def _():
            send_x(step, (4, 6))

        send_x(step, (2,))
        own_x(step).start()

    loop(0, steps, first)

    a_copy(0, True).wait_recv()
    a_copy(2).start()
    a_copy(4).start()

    def forward(step):
        for k in (1, 3):
            x_copy(step, k, True).wait_recv()
            x_copy(step, k + 4).start()

        @pl.when(step + AHEAD < steps)
        def _():
            send_x(step + AHEAD, (4, 6))

    def multiply(step):
        own_x(step).wait()
        for k in (2, 4, 6, 5, 7):
            x_copy(step, k, True).wait_recv()
        for n, k in enumerate((1, 3, 2, 0)):
            at = pl.ds(pl.multiple_of(in_side(k) * rows, rows), rows)
            acc = jnp.dot(a_buf[at, :], x_buf[step], preferred_element_type=jnp.float32)
            y_buf[step, at, :] = acc.astype(y_buf.dtype)
            if n:
                y_copy(step, (1, 3, 2)[n - 1]).start()

    loop(0, LAG, forward)
    a_copy(1, True).wait_recv()
    a_copy(5).start()
    a_copy(2, True).wait_recv()
    a_copy(6).start()
    own_a.wait()
    for n in (3, 4, 5, 6):
        a_copy(n, True).wait_recv()

    def both(step):
        forward(step)
        multiply(step - LAG)

    loop(LAG, steps, both)
    loop(steps - LAG, steps, multiply)

    for n in range(7):
        a_copy(n).wait_send()

    def x_done(step):
        for k in range(1, BLOCKS):
            x_copy(step, k).wait_send()
        own_y(step).start()

    loop(0, steps, x_done)

    def y_done(step):
        for k in (1, 3, 2):
            y_copy(step, k).wait_send()
            y_copy(step, k, True).wait_recv()
        own_y(step).wait()

    loop(0, steps, y_done)


def solution(mesh):
    def local(w, x):
        rhs, rows, cols = x.shape
        n = rows * BLOCKS
        steps = rhs * (cols // SIDE // PIECE)
        sems = pltpu.SemaphoreType.DMA
        return pl.pallas_call(
            kernel,
            out_shape=pltpu.VMEM(x.shape, x.dtype),
            in_specs=[pl.BlockSpec(memory_space=pl.ANY)] * 2,
            out_specs=pl.BlockSpec(memory_space=pltpu.VMEM),
            scratch_shapes=[
                pltpu.VMEM((SIDE * rows, n), w.dtype),
                pltpu.VMEM((steps, n, PIECE), x.dtype),
                pltpu.VMEM((steps, SIDE * rows, PIECE), x.dtype),
                sems((7,)), sems((7,)),
                sems((steps, BLOCKS)), sems((steps, BLOCKS)),
                sems((steps, SIDE)), sems((steps, SIDE)),
                sems((3, steps)),
            ],
            compiler_params=pltpu.CompilerParams(collective_id=0, has_side_effects=True, vmem_limit_bytes=52 * 1024 * 1024),
        )(w, x)

    return jax.shard_map(local, mesh=mesh, in_specs=(P(("row", "depth"), "col"), P(None, ("row", "depth"), "col")),
                         out_specs=P(None, ("row", "depth"), "col"), check_vma=False)
```

time: 338 us -> 157 us (0.46)
  blocking collectives: 218 us -> 0 us
  Pallas kernels: 0 us -> 154 us
  local copies, waits for them, and re-layouts: 62.6 us -> 2.71 us
  waiting for transfers between devices: 24.3 us -> 0 us
  matrix products: 18.9 us -> 0 us
  between operations: 13.4 us -> 0.01 us
    all_to_all x2 -> x0, blocking collectives: 218 us -> none  [the longest x1 121 us: local(): xs = lax.all_to_all(x, plane, split_axis=2, concat_axis=1, tiled=True)]
    pallas_call x0 -> x1, Pallas kernels: none -> 154 us  [local(): pl.pallas_call(kernel, out_shape=pltpu.VMEM(x.shape, x.dtype), in_specs=[...]
    all_to_all x4 -> x0, local copies, waits for them, and re-layouts: 35.5 us -> none  [the longest x2 17.8 us: local(): xs = lax.all_to_all(x, plane, split_axis=2, concat_axis=1, tiled=True)]
    all_gather x2 -> x0, waiting for transfers between devices: 23.6 us -> none  [the longest x1 23.6 us: local(): w = lax.all_gather(w, 'col', axis=1, tiled=True)]
    dot_general x1 -> x0, matrix products: 18.9 us -> none  [local(): jnp.einsum('mk,rkn->rmn', w, xs, preferred_element_type=jnp.float32)]
    convert_element_type x1 -> x0, local copies, waits for them, and re-layouts: 14.1 us -> none  [local(): jnp.einsum('mk,rkn->rmn', w, xs, preferred_element_type=jnp.float32)]
    unnamed x1, local copies, waits for them, and re-layouts: 13.1 us -> 2.71 us
  transfers between devices with their start and end apart: 2 -> 0, of which waited for: 1 -> 0; matrix products, arithmetic and copies ran while one was open for 6% -> 0% of each run, Pallas kernels for 0% -> 0%
where the time goes in v3:
time: 157 us
  Pallas kernels  154 us (98%)
  local copies, waits for them, and re-layouts  2.71 us (2%)
    pallas_call x1, Pallas kernels, local(): pl.pallas_call(kernel, out_shape=pltpu.VMEM(x.shape, x.dtype), in_specs=[...  154 us

profile of v3, /device:TPU:0, one launch (start us, length us, event | category | flops | bytes accessed | tf_op | source)
XLA Modules:
  0.0 157.0 jit_solution(5875920657491037997)
XLA Ops:
  0.0 154.3 %shard_map.28 = bf16[3,256,4096]{2,1,0:T(8,128)(2,1)S(1)} custom-call(bf16[256,1024]{1,0:T(8,128)(2,1)} %w_ref.1, bf16[3,256,4096]{2,1,0:T(8,128)(2,1)} %x_ref.1), custom_call_target="tpu_custom_call" | custom-call | tf_op jit(solution)/shard_map/pallas_call | solution.py:188
  154.3 2.7 %copy.4 = bf16[3,256,4096]{2,1,0:T(8,128)(2,1)} copy(bf16[3,256,4096]{2,1,0:T(8,128)(2,1)S(1)} %shard_map.28) | data formatting | bytes 12582912

commit v4 on v1

v4 whole, which is shorter than its diff:
```python
import jax
import jax.numpy as jnp
from jax import lax
from jax.experimental import pallas as pl
from jax.experimental.pallas import tpu as pltpu
from jax.sharding import PartitionSpec as P

MESH = pl.DeviceIdType.MESH
SIDE = 4
PIECES = ((0, 0, 512), (0, 512, 512), (1, 0, 512), (1, 512, 512), (2, 0, 512), (2, 512, 256), (2, 768, 256))
DIRECT = ((0, 0, 1024), (1, 0, 1024), (2, 0, 512), (2, 512, 512))
WIDE = 256


def kernel(w_ref, x_ref, y_ref, a_buf, x_buf, y_buf, a_send, a_recv, z_send, z_recv, d_send, d_recv, f_send, f_recv,
           p_send, p_recv, y_send, y_recv, q_send, q_recv, own_sem):
    z, j, row = lax.axis_index("depth"), lax.axis_index("col"), lax.axis_index("row")
    x, c = row // 2, row % 2
    rhs, rows, cols = x_ref.shape
    kcols = w_ref.shape[1]
    group = cols // SIDE

    def peer(k):
        kx, kc, kz = k // 4 % 2, k // 2 % 2, k % 2
        return x + kx * (1 - 2 * x), c + kc * (1 - 2 * c), z + kz * (1 - 2 * z)

    def device(k):
        px, pc, pz = peer(k)
        return (pz, j, px * 2 + pc)

    def in_side(k):
        _, pc, pz = peer(k)
        return pc * 2 + pz

    other_y = (z, 1 - j, row)

    def remote(src, dst, send, recv, to):
        return pltpu.make_async_remote_copy(src, dst, send, recv, device_id=to, device_id_type=MESH)

    def a_rows(k):
        return pl.ds(pl.multiple_of(in_side(k) * rows, rows), rows)

    def a_block(k, jj):
        return a_buf.at[a_rows(k), pl.ds(pl.multiple_of(jj * kcols, kcols), kcols)]

    def a_copy(n, receive=False):
        own = (w_ref, a_block(0, j))
        src, there, here, to = (
            own + (a_block(1, j), device(1)),
            own + (a_block(0, 1 - j), other_y),
            (a_block(1, j),) * 2 + (a_block(1, 1 - j), other_y),
            own + (a_block(2, j), device(2)),
            (a_block(1, j),) * 2 + (a_block(3, j), device(2)),
            (a_block(0, 1 - j),) * 2 + (a_block(2, 1 - j), device(2)),
            (a_block(1, 1 - j),) * 2 + (a_block(3, 1 - j), device(2)),
        )[n]
        return remote(src, here if receive else there, a_send.at[n], a_recv.at[n], to)

    def given(piece, k):
        r, at, width = piece
        return (r, slice(None), pl.ds(pl.multiple_of(in_side(k) * group + at, WIDE), width))

    def held(piece, k):
        r, at, width = piece
        px, pc, pz = peer(k)
        return x_buf.at[r, px, pc, pz, :, pl.ds(at, width)]

    def x_copy(piece, k, send, recv, receive=False):
        return remote(x_ref.at[given(piece, k)], held(piece, k if receive else 0), send, recv, device(k))

    def z_copy(n, i, receive=False):
        return x_copy(PIECES[n], (1, 3)[i], z_send.at[n, i], z_recv.at[n, i], receive)

    def d_copy(n, i, receive=False):
        return x_copy(DIRECT[n], (4, 6)[i], d_send.at[n, i], d_recv.at[n, i], receive)

    def f_copy(n, receive=False):
        r, at, width = PIECES[n]
        src = x_buf.at[r, x, :, 1 - z, :, pl.ds(at, width)]
        here = x_buf.at[r, 1 - x, :, 1 - z, :, pl.ds(at, width)]
        return remote(src, here if receive else src, f_send.at[n], f_recv.at[n], device(4))

    everything = (slice(None), 0, group)

    def p_copy(receive=False):
        return x_copy(everything, 2, p_send.at[0], p_recv.at[0], receive)

    def y_copy(n, kc, receive=False):
        k = kc * 2 + 1
        r, at, width = PIECES[n]
        src = y_buf.at[r, a_rows(k), pl.ds(at, width)]
        return remote(src, y_ref.at[given(PIECES[n], k if receive else 0)], y_send.at[n, kc], y_recv.at[n, kc], device(k))

    def q_copy(r, receive=False):
        piece = (r, 0, group)
        return remote(y_buf.at[r, a_rows(2), :], y_ref.at[given(piece, 2 if receive else 0)], q_send.at[r], q_recv.at[r], device(2))

    own_a = pltpu.make_async_copy(w_ref, a_block(0, j), own_sem.at[0])
    own_x = pltpu.make_async_copy(x_ref.at[given(everything, 0)], held(everything, 0), own_sem.at[1])

    def product(k, r, at):
        xs = x_buf[r, :, :, :, :, pl.ds(at, WIDE)].reshape(-1, WIDE)
        return jnp.dot(a_buf[a_rows(k), :], xs, preferred_element_type=jnp.float32).astype(y_buf.dtype)

    def forward(n):
        for i in range(2):
            z_copy(n, i, True).wait_recv()
        f_copy(n).start()

    def direct(n):
        for i in range(2):
            d_copy(n, i).start()

    def multiply(n):
        r, at, width = PIECES[n]
        for m, piece in enumerate(DIRECT):
            if piece[:2] == (r, at):
                for i in range(2):
                    d_copy(m, i, True).wait_recv()
        f_copy(n, True).wait_recv()
        parts = width // WIDE

        def tile(s, carry):
            t, at_s = s // parts, at + s % parts * WIDE
            kz = 1 - t // 2
            k = (t % 2 + t // 2) % 2 * 2 + kz
            at_s = pl.multiple_of(at_s, WIDE)
            y_buf[r, a_rows(k), pl.ds(at_s, WIDE)] = product(k, r, at_s)

            @pl.when(s % parts == 0)
            def _():
                for i in range(2):
                    @pl.when(t == i + 1)
                    def _():
                        y_copy(n, i).start()

            return carry

        lax.fori_loop(0, 3 * parts, tile, 0)

        def own(s, carry):
            at_s = pl.multiple_of(at + s * WIDE, WIDE)
            y_ref[r, :, pl.ds(pl.multiple_of(in_side(0) * group + at_s, WIDE), WIDE)] = product(0, r, at_s)
            return carry

        lax.fori_loop(0, parts, own, 0)
        if at + width == group:
            q_copy(r).start()

    barrier = pltpu.get_barrier_semaphore()
    for to in [device(k) for k in (1, 2, 3, 4, 6)] + [other_y]:
        pl.semaphore_signal(barrier, inc=1, device_id=to, device_id_type=MESH)
    pl.semaphore_wait(barrier, 6)

    a_copy(0).start()
    direct(0)
    a_copy(1).start()
    for n in range(len(PIECES)):
        for i in range(2):
            z_copy(n, i).start()
    direct(1)
    a_copy(3).start()
    own_a.start()
    p_copy().start()
    own_x.start()

    a_copy(0, True).wait_recv()
    a_copy(2).start()
    a_copy(4).start()
    a_copy(1, True).wait_recv()
    a_copy(5).start()
    forward(0)
    a_copy(2, True).wait_recv()
    a_copy(6).start()
    forward(1)
    own_a.wait()
    for n in (3, 4, 5, 6):
        a_copy(n, True).wait_recv()
    own_x.wait()
    p_copy(True).wait_recv()
    forward(2)
    multiply(0)
    forward(3)
    direct(2)
    multiply(1)
    forward(4)
    direct(3)
    multiply(2)
    forward(5)
    forward(6)
    for n in range(3, len(PIECES)):
        multiply(n)

    for n in range(7):
        a_copy(n).wait_send()
    p_copy().wait_send()
    for n in range(len(DIRECT)):
        for i in range(2):
            d_copy(n, i).wait_send()
    for n in range(len(PIECES)):
        f_copy(n).wait_send()
        for i in range(2):
            z_copy(n, i).wait_send()
    for r in range(rhs):
        q_copy(r).wait_send()
        q_copy(r, True).wait_recv()
    for n in range(len(PIECES)):
        for i in range(2):
            y_copy(n, i).wait_send()
            y_copy(n, i, True).wait_recv()


def solution(mesh):
    def local(w, x):
        rhs, rows, cols = x.shape
        n = w.shape[1] * 2
        sems = []
        for shape in ((7,), (len(PIECES), 2), (len(DIRECT), 2), (len(PIECES),), (1,), (len(PIECES), 2), (rhs,)):
            sems += [pltpu.SemaphoreType.DMA(shape)] * 2
        return pl.pallas_call(
            kernel,
            out_shape=pltpu.VMEM(x.shape, x.dtype),
            in_specs=[pl.BlockSpec(memory_space=pl.ANY)] * 2,
            out_specs=pl.BlockSpec(memory_space=pltpu.VMEM),
            scratch_shapes=[
                pltpu.VMEM((SIDE * rows, n), w.dtype),
                pltpu.VMEM((rhs, 2, 2, 2, rows, cols // SIDE), x.dtype),
                pltpu.VMEM((rhs, SIDE * rows, cols // SIDE), x.dtype),
                *sems,
                pltpu.SemaphoreType.DMA((2,)),
            ],
            compiler_params=pltpu.CompilerParams(collective_id=0, has_side_effects=True, vmem_limit_bytes=52 * 1024 * 1024),
        )(w, x)

    return jax.shard_map(local, mesh=mesh, in_specs=(P(("row", "depth"), "col"), P(None, ("row", "depth"), "col")),
                         out_specs=P(None, ("row", "depth"), "col"), check_vma=False)
```

time: 338 us -> 155 us (0.46)
  blocking collectives: 218 us -> 0 us
  Pallas kernels: 0 us -> 152 us
  local copies, waits for them, and re-layouts: 62.6 us -> 2.71 us
  waiting for transfers between devices: 24.3 us -> 0 us
  matrix products: 18.9 us -> 0 us
  between operations: 13.4 us -> 0.01 us
    all_to_all x2 -> x0, blocking collectives: 218 us -> none  [the longest x1 121 us: local(): xs = lax.all_to_all(x, plane, split_axis=2, concat_axis=1, tiled=True)]
    pallas_call x0 -> x1, Pallas kernels: none -> 152 us  [local(): pl.pallas_call(kernel, out_shape=pltpu.VMEM(x.shape, x.dtype), in_specs=[...]
    all_to_all x4 -> x0, local copies, waits for them, and re-layouts: 35.5 us -> none  [the longest x2 17.8 us: local(): xs = lax.all_to_all(x, plane, split_axis=2, concat_axis=1, tiled=True)]
    all_gather x2 -> x0, waiting for transfers between devices: 23.6 us -> none  [the longest x1 23.6 us: local(): w = lax.all_gather(w, 'col', axis=1, tiled=True)]
    dot_general x1 -> x0, matrix products: 18.9 us -> none  [local(): jnp.einsum('mk,rkn->rmn', w, xs, preferred_element_type=jnp.float32)]
    convert_element_type x1 -> x0, local copies, waits for them, and re-layouts: 14.1 us -> none  [local(): jnp.einsum('mk,rkn->rmn', w, xs, preferred_element_type=jnp.float32)]
    unnamed x1, local copies, waits for them, and re-layouts: 13.1 us -> 2.71 us
  transfers between devices with their start and end apart: 2 -> 0, of which waited for: 1 -> 0; matrix products, arithmetic and copies ran while one was open for 6% -> 0% of each run, Pallas kernels for 0% -> 0%
where the time goes in v4:
time: 155 us
  Pallas kernels  152 us (98%)
  local copies, waits for them, and re-layouts  2.71 us (2%)
    pallas_call x1, Pallas kernels, local(): pl.pallas_call(kernel, out_shape=pltpu.VMEM(x.shape, x.dtype), in_specs=[...  152 us

profile of v4, /device:TPU:0, one launch (start us, length us, event | category | flops | bytes accessed | tf_op | source)
XLA Modules:
  0.0 154.9 jit_solution(14958651441061936467)
XLA Ops:
  0.0 152.2 %shard_map.28 = bf16[3,256,4096]{2,1,0:T(8,128)(2,1)S(1)} custom-call(bf16[256,1024]{1,0:T(8,128)(2,1)} %w_ref.1, bf16[3,256,4096]{2,1,0:T(8,128)(2,1)} %x_ref.1), custom_call_target="tpu_custom_call" | custom-call | tf_op jit(solution)/shard_map/pallas_call | solution.py:220
  152.2 2.7 %copy.4 = bf16[3,256,4096]{2,1,0:T(8,128)(2,1)} copy(bf16[3,256,4096]{2,1,0:T(8,128)(2,1)S(1)} %shard_map.28) | data formatting | bytes 12582912

commit v5 on v4

--- a/solution.py
+++ b/solution.py
@@ -7,8 +7,8 @@
 
 MESH = pl.DeviceIdType.MESH
 SIDE = 4
-PIECES = ((0, 0, 512), (0, 512, 512), (1, 0, 512), (1, 512, 512), (2, 0, 512), (2, 512, 256), (2, 768, 256))
-DIRECT = ((0, 0, 1024), (1, 0, 1024), (2, 0, 512), (2, 512, 512))
+PIECES = ((0, 0, 1024), (1, 0, 1024), (2, 0, 512), (2, 512, 256), (2, 768, 256))
+SPLIT = (0, 1)
 WIDE = 256
 
 
@@ -71,14 +71,22 @@
     def z_copy(n, i, receive=False):
         return x_copy(PIECES[n], (1, 3)[i], z_send.at[n, i], z_recv.at[n, i], receive)
 
-    def d_copy(n, i, receive=False):
-        return x_copy(DIRECT[n], (4, 6)[i], d_send.at[n, i], d_recv.at[n, i], receive)
+    def along_x(piece, side, send, recv, receive):
+        r, at, width = piece
+        src, here = (x_buf.at[r, px, :, side, :, pl.ds(at, width)] for px in (x, 1 - x))
+        return remote(src, here if receive else src, send, recv, device(4))
+
+    def d_copy(n, receive=False):
+        if n == 0:
+            return x_copy((0, 0, group), 4, d_send.at[n], d_recv.at[n], receive)
+        if n == 1:
+            src, here = (x_buf.at[0, px, 1 - c, z] for px in (x, 1 - x))
+            return remote(src, here if receive else src, d_send.at[n], d_recv.at[n], device(4))
+        return along_x((n - 1, 0, group), z, d_send.at[n], d_recv.at[n], receive)
 
     def f_copy(n, receive=False):
-        r, at, width = PIECES[n]
-        src = x_buf.at[r, x, :, 1 - z, :, pl.ds(at, width)]
-        here = x_buf.at[r, 1 - x, :, 1 - z, :, pl.ds(at, width)]
-        return remote(src, here if receive else src, f_send.at[n], f_recv.at[n], device(4))
+        side = 1 - z if PIECES[n][0] in SPLIT else slice(None)
+        return along_x(PIECES[n], side, f_send.at[n], f_recv.at[n], receive)
 
     everything = (slice(None), 0, group)
 
@@ -91,9 +99,10 @@
         src = y_buf.at[r, a_rows(k), pl.ds(at, width)]
         return remote(src, y_ref.at[given(PIECES[n], k if receive else 0)], y_send.at[n, kc], y_recv.at[n, kc], device(k))
 
-    def q_copy(r, receive=False):
+    def q_copy(n, receive=False):
+        r = (pl.ds(0, rhs - 1), pl.ds(rhs - 1, 1))[n]
         piece = (r, 0, group)
-        return remote(y_buf.at[r, a_rows(2), :], y_ref.at[given(piece, 2 if receive else 0)], q_send.at[r], q_recv.at[r], device(2))
+        return remote(y_buf.at[r, a_rows(2), :], y_ref.at[given(piece, 2 if receive else 0)], q_send.at[n], q_recv.at[n], device(2))
 
     own_a = pltpu.make_async_copy(w_ref, a_block(0, j), own_sem.at[0])
     own_x = pltpu.make_async_copy(x_ref.at[given(everything, 0)], held(everything, 0), own_sem.at[1])
@@ -107,16 +116,11 @@
             z_copy(n, i, True).wait_recv()
         f_copy(n).start()
 
-    def direct(n):
-        for i in range(2):
-            d_copy(n, i).start()
-
     def multiply(n):
         r, at, width = PIECES[n]
-        for m, piece in enumerate(DIRECT):
-            if piece[:2] == (r, at):
-                for i in range(2):
-                    d_copy(m, i, True).wait_recv()
+        if r in SPLIT and at == 0:
+            for m in (0, 1) if r == 0 else (r + 1,):
+                d_copy(m, True).wait_recv()
         f_copy(n, True).wait_recv()
         parts = width // WIDE
 
@@ -144,68 +148,61 @@
             return carry
 
         lax.fori_loop(0, parts, own, 0)
-        if at + width == group:
-            q_copy(r).start()
+        if at + width == group and r >= rhs - 2:
+            q_copy(r - rhs + 2).start()
 
     barrier = pltpu.get_barrier_semaphore()
-    for to in [device(k) for k in (1, 2, 3, 4, 6)] + [other_y]:
+    for to in [device(k) for k in (1, 2, 3, 4)] + [other_y]:
         pl.semaphore_signal(barrier, inc=1, device_id=to, device_id_type=MESH)
-    pl.semaphore_wait(barrier, 6)
+    pl.semaphore_wait(barrier, 5)
 
     a_copy(0).start()
-    direct(0)
+    d_copy(0).start()
+    p_copy().start()
+    own_x.start()
     a_copy(1).start()
     for n in range(len(PIECES)):
         for i in range(2):
             z_copy(n, i).start()
-    direct(1)
     a_copy(3).start()
     own_a.start()
-    p_copy().start()
-    own_x.start()
-
+
+    own_x.wait()
+    p_copy(True).wait_recv()
+    for n in range(1, len(SPLIT) + 1):
+        d_copy(n).start()
     a_copy(0, True).wait_recv()
     a_copy(2).start()
     a_copy(4).start()
     a_copy(1, True).wait_recv()
     a_copy(5).start()
-    forward(0)
     a_copy(2, True).wait_recv()
     a_copy(6).start()
-    forward(1)
     own_a.wait()
     for n in (3, 4, 5, 6):
         a_copy(n, True).wait_recv()
-    own_x.wait()
-    p_copy(True).wait_recv()
+    forward(0)
+    forward(1)
+    multiply(0)
     forward(2)
-    multiply(0)
+    multiply(1)
     forward(3)
-    direct(2)
-    multiply(1)
     forward(4)
-    direct(3)
-    multiply(2)
-    forward(5)
-    forward(6)
-    for n in range(3, len(PIECES)):
+    for n in range(2, len(PIECES)):
         multiply(n)
 
     for n in range(7):
         a_copy(n).wait_send()
     p_copy().wait_send()
-    for n in range(len(DIRECT)):
-        for i in range(2):
-            d_copy(n, i).wait_send()
+    for n in range(len(SPLIT) + 1):
+        d_copy(n).wait_send()
+    for n in range(2):
+        q_copy(n).wait_send()
+        q_copy(n, True).wait_recv()
     for n in range(len(PIECES)):
         f_copy(n).wait_send()
         for i in range(2):
             z_copy(n, i).wait_send()
-    for r in range(rhs):
-        q_copy(r).wait_send()
-        q_copy(r, True).wait_recv()
-    for n in range(len(PIECES)):
-        for i in range(2):
             y_copy(n, i).wait_send()
             y_copy(n, i, True).wait_recv()
 
@@ -215,7 +212,7 @@
         rhs, rows, cols = x.shape
         n = w.shape[1] * 2
         sems = []
-        for shape in ((7,), (len(PIECES), 2), (len(DIRECT), 2), (len(PIECES),), (1,), (len(PIECES), 2), (rhs,)):
+        for shape in ((7,), (len(PIECES), 2), (len(SPLIT) + 1,), (len(PIECES),), (1,), (len(PIECES), 2), (2,)):
             sems += [pltpu.SemaphoreType.DMA(shape)] * 2
         return pl.pallas_call(
             kernel,

time: 155 us -> 154 us (level)
  no operation moved by 1% of the time
where the time goes in v5:
time: 154 us
  Pallas kernels  151 us (98%)
  local copies, waits for them, and re-layouts  2.71 us (2%)
    pallas_call x1, Pallas kernels, local(): pl.pallas_call(kernel, out_shape=pltpu.VMEM(x.shape, x.dtype), in_specs=[...  151 us

profile of v5, /device:TPU:0, one launch (start us, length us, event | category | flops | bytes accessed | tf_op | source)
XLA Modules:
  0.0 153.6 jit_solution(330438865036314250)
XLA Ops:
  0.0 150.9 %shard_map.28 = bf16[3,256,4096]{2,1,0:T(8,128)(2,1)S(1)} custom-call(bf16[256,1024]{1,0:T(8,128)(2,1)} %w_ref.1, bf16[3,256,4096]{2,1,0:T(8,128)(2,1)} %x_ref.1), custom_call_target="tpu_custom_call" | custom-call | tf_op jit(solution)/shard_map/pallas_call | solution.py:217
  150.9 2.7 %copy.4 = bf16[3,256,4096]{2,1,0:T(8,128)(2,1)} copy(bf16[3,256,4096]{2,1,0:T(8,128)(2,1)S(1)} %shard_map.28) | data formatting | bytes 12582912

commit v6 on v5

v6 whole, which is shorter than its diff:
```python
import jax
import jax.numpy as jnp
from jax import lax
from jax.experimental import pallas as pl
from jax.experimental.pallas import tpu as pltpu
from jax.sharding import PartitionSpec as P

MESH = pl.DeviceIdType.MESH
SIDE = 4
PIECES = ((0, 0, 1024), (1, 0, 1024), (2, 0, 512), (2, 512, 256), (2, 768, 256))
SPLIT = 2
WIDE = 256


def kernel(w_ref, x_ref, y_ref, a_buf, x_buf, y_buf, a_send, a_recv, z_send, z_recv, d_send, d_recv, f_send, f_recv,
           p_send, p_recv, y_send, y_recv, q_send, q_recv, own_sem):
    z, j, row = lax.axis_index("depth"), lax.axis_index("col"), lax.axis_index("row")
    x, c = row // 2, row % 2
    rhs, rows, cols = x_ref.shape
    kcols = w_ref.shape[1]
    group = cols // SIDE

    def peer(k):
        kx, kc, kz = k // 4 % 2, k // 2 % 2, k % 2
        return x + kx * (1 - 2 * x), c + kc * (1 - 2 * c), z + kz * (1 - 2 * z)

    def device(k):
        px, pc, pz = peer(k)
        return (pz, j, px * 2 + pc)

    def in_side(k):
        _, pc, pz = peer(k)
        return pc * 2 + pz

    other_y = (z, 1 - j, row)

    def remote(src, dst, send, recv, to):
        return pltpu.make_async_remote_copy(src, dst, send, recv, device_id=to, device_id_type=MESH)

    def a_block(k, jj):
        _, pc, pz = peer(k)
        return a_buf.at[pc, pz, :, pl.ds(pl.multiple_of(jj * kcols, kcols), kcols)]

    def rows_of(k):
        return pl.ds(pl.multiple_of(in_side(k) * rows, rows), rows)

    def a_copy(n, receive=False):
        if n == 0:
            src, here, to = w_ref, a_block(1, j), device(1)
            there = a_block(0, j)
        elif n == 1:
            there, here = (a_buf.at[c, :, :, pl.ds(pl.multiple_of(jj * kcols, kcols), kcols)] for jj in (j, 1 - j))
            src, to = there, other_y
        else:
            there, here = a_buf.at[c], a_buf.at[1 - c]
            src, to = there, device(2)
        return remote(src, here if receive else there, a_send.at[n], a_recv.at[n], to)

    def given(piece, k):
        r, at, width = piece
        return (r, slice(None), pl.ds(pl.multiple_of(in_side(k) * group + at, WIDE), width))

    def held(piece, k):
        r, at, width = piece
        px, pc, pz = peer(k)
        return x_buf.at[r, px, pc, pz, :, pl.ds(at, width)]

    def x_copy(piece, k, send, recv, receive=False):
        return remote(x_ref.at[given(piece, k)], held(piece, k if receive else 0), send, recv, device(k))

    def z_copy(r, i, receive=False):
        return x_copy((r, 0, group), (1, 3)[i], z_send.at[r, i], z_recv.at[r, i], receive)

    def along_x(piece, side, send, recv, receive):
        r, at, width = piece
        src, here = (x_buf.at[r, px, :, side, :, pl.ds(at, width)] for px in (x, 1 - x))
        return remote(src, here if receive else src, send, recv, device(4))

    ahead = (pl.ds(0, SPLIT), 0, group)

    def d_copy(n, receive=False):
        if n == 0:
            return x_copy(ahead, 4, d_send.at[n], d_recv.at[n], receive)
        src, here = (x_buf.at[ahead[0], px, 1 - c, z] for px in (x, 1 - x))
        return remote(src, here if receive else src, d_send.at[n], d_recv.at[n], device(4))

    def f_copy(n, receive=False):
        side = 1 - z if PIECES[n][0] < SPLIT else slice(None)
        return along_x(PIECES[n], side, f_send.at[n], f_recv.at[n], receive)

    everything = (slice(None), 0, group)

    def p_copy(receive=False):
        return x_copy(everything, 2, p_send.at[0], p_recv.at[0], receive)

    def y_copy(n, kc, receive=False):
        k = kc * 2 + 1
        r, at, width = PIECES[n]
        src = y_buf.at[r, rows_of(k), pl.ds(at, width)]
        return remote(src, y_ref.at[given(PIECES[n], k if receive else 0)], y_send.at[n, kc], y_recv.at[n, kc], device(k))

    def q_copy(receive=False):
        there = y_ref.at[given(everything, 2 if receive else 0)]
        return remote(y_buf.at[:, rows_of(2), :], there, q_send.at[0], q_recv.at[0], device(2))

    own_a = pltpu.make_async_copy(w_ref, a_block(0, j), own_sem.at[0])
    own_x = pltpu.make_async_copy(x_ref.at[given(everything, 0)], held(everything, 0), own_sem.at[1])

    def product(k, r, at):
        xs = x_buf[r, :, :, :, :, pl.ds(at, WIDE)].reshape(-1, WIDE)
        return jnp.dot(a_buf[peer(k)[1], peer(k)[2]], xs, preferred_element_type=jnp.float32).astype(y_buf.dtype)

    def forward(n):
        r, at, _ = PIECES[n]
        if at == 0:
            for i in range(2):
                z_copy(r, i, True).wait_recv()
        f_copy(n).start()

    def multiply(n):
        r, at, width = PIECES[n]
        if n == 0:
            for m in range(2):
                d_copy(m, True).wait_recv()
        f_copy(n, True).wait_recv()
        parts = width // WIDE

        def tile(s, carry):
            t, at_s = s // parts, at + s % parts * WIDE
            kz = 1 - t // 2
            k = (t % 2 + t // 2) % 2 * 2 + kz
            at_s = pl.multiple_of(at_s, WIDE)
            y_buf[r, rows_of(k), pl.ds(at_s, WIDE)] = product(k, r, at_s)

            @pl.when(s % parts == 0)
            def _():
                for i in range(2):
                    @pl.when(t == i + 1)
                    def _():
                        y_copy(n, i).start()

            return carry

        lax.fori_loop(0, 3 * parts, tile, 0)

        def own(s, carry):
            at_s = pl.multiple_of(at + s * WIDE, WIDE)
            y_ref[r, :, pl.ds(pl.multiple_of(in_side(0) * group + at_s, WIDE), WIDE)] = product(0, r, at_s)
            return carry

        lax.fori_loop(0, parts, own, 0)

    barrier = pltpu.get_barrier_semaphore()
    for to in [device(k) for k in (1, 2, 3, 4)] + [other_y]:
        pl.semaphore_signal(barrier, inc=1, device_id=to, device_id_type=MESH)
    pl.semaphore_wait(barrier, 5)

    a_copy(0).start()
    d_copy(0).start()
    p_copy().start()
    own_x.start()
    for r in range(rhs):
        for i in range(2):
            z_copy(r, i).start()
    own_a.start()

    own_x.wait()
    p_copy(True).wait_recv()
    d_copy(1).start()
    own_a.wait()
    a_copy(0, True).wait_recv()
    a_copy(1).start()
    a_copy(1, True).wait_recv()
    a_copy(2).start()
    a_copy(2, True).wait_recv()
    forward(0)
    forward(1)
    multiply(0)
    forward(2)
    multiply(1)
    forward(3)
    forward(4)
    for n in range(2, len(PIECES)):
        multiply(n)

    q_copy().start()
    for n in range(3):
        a_copy(n).wait_send()
    p_copy().wait_send()
    for n in range(2):
        d_copy(n).wait_send()
    for r in range(rhs):
        for i in range(2):
            z_copy(r, i).wait_send()
    q_copy().wait_send()
    q_copy(True).wait_recv()
    for n in range(len(PIECES)):
        f_copy(n).wait_send()
        for i in range(2):
            y_copy(n, i).wait_send()
            y_copy(n, i, True).wait_recv()


def solution(mesh):
    def local(w, x):
        rhs, rows, cols = x.shape
        sems = []
        for shape in ((3,), (rhs, 2), (2,), (len(PIECES),), (1,), (len(PIECES), 2), (1,)):
            sems += [pltpu.SemaphoreType.DMA(shape)] * 2
        return pl.pallas_call(
            kernel,
            out_shape=pltpu.VMEM(x.shape, x.dtype),
            in_specs=[pl.BlockSpec(memory_space=pl.ANY)] * 2,
            out_specs=pl.BlockSpec(memory_space=pltpu.VMEM),
            scratch_shapes=[
                pltpu.VMEM((2, 2, rows, w.shape[1] * 2), w.dtype),
                pltpu.VMEM((rhs, 2, 2, 2, rows, cols // SIDE), x.dtype),
                pltpu.VMEM((rhs, SIDE * rows, cols // SIDE), x.dtype),
                *sems,
                pltpu.SemaphoreType.DMA((2,)),
            ],
            compiler_params=pltpu.CompilerParams(collective_id=0, has_side_effects=True, vmem_limit_bytes=52 * 1024 * 1024),
        )(w, x)

    return jax.shard_map(local, mesh=mesh, in_specs=(P(("row", "depth"), "col"), P(None, ("row", "depth"), "col")),
                         out_specs=P(None, ("row", "depth"), "col"), check_vma=False)
```

time: 154 us -> 154 us (level)
  no operation moved by 1% of the time
where the time goes in v6:
time: 154 us; the launch traced here: 153 us
  Pallas kernels  151 us (98%)
  local copies, waits for them, and re-layouts  2.71 us (2%)
    pallas_call x1, Pallas kernels, local(): pl.pallas_call(kernel, out_shape=pltpu.VMEM(x.shape, x.dtype), in_specs=[...  151 us

profile of v6, /device:TPU:0, one launch (start us, length us, event | category | flops | bytes accessed | tf_op | source)
XLA Modules:
  0.0 153.4 jit_solution(8759940543291908698)
XLA Ops:
  0.0 150.7 %shard_map.28 = bf16[3,256,4096]{2,1,0:T(8,128)(2,1)S(1)} custom-call(bf16[256,1024]{1,0:T(8,128)(2,1)} %w_ref.1, bf16[3,256,4096]{2,1,0:T(8,128)(2,1)} %x_ref.1), custom_call_target="tpu_custom_call" | custom-call | tf_op jit(solution)/shard_map/pallas_call | solution.py:210
  150.7 2.7 %copy.4 = bf16[3,256,4096]{2,1,0:T(8,128)(2,1)} copy(bf16[3,256,4096]{2,1,0:T(8,128)(2,1)S(1)} %shard_map.28) | data formatting | bytes 12582912

commit v7 on v6

--- a/solution.py
+++ b/solution.py
@@ -13,7 +13,7 @@
 
 
 def kernel(w_ref, x_ref, y_ref, a_buf, x_buf, y_buf, a_send, a_recv, z_send, z_recv, d_send, d_recv, f_send, f_recv,
-           p_send, p_recv, y_send, y_recv, q_send, q_recv, own_sem):
+           p_send, p_recv, y_send, y_recv, q_send, q_recv, own_sem, ready):
     z, j, row = lax.axis_index("depth"), lax.axis_index("col"), lax.axis_index("row")
     x, c = row // 2, row % 2
     rhs, rows, cols = x_ref.shape
@@ -151,18 +151,42 @@
         lax.fori_loop(0, parts, own, 0)
 
     barrier = pltpu.get_barrier_semaphore()
-    for to in [device(k) for k in (1, 2, 3, 4)] + [other_y]:
-        pl.semaphore_signal(barrier, inc=1, device_id=to, device_id_type=MESH)
-    pl.semaphore_wait(barrier, 5)
+    for k in (1, 3):
+        pl.semaphore_signal(barrier, inc=1, device_id=device(k), device_id_type=MESH)
+
+    @pl.when(z == 0)
+    def _():
+        for to in (device(2), device(4), other_y):
+            pl.semaphore_signal(barrier, inc=1, device_id=to, device_id_type=MESH)
+        pl.semaphore_wait(barrier, 5)
+        for to in (device(4), other_y):
+            pl.semaphore_signal(ready, inc=1, device_id=to, device_id_type=MESH)
+
+    @pl.when(z == 1)
+    def _():
+        pl.semaphore_wait(barrier, 2)
+
+    def beside_z():
+        d_copy(0).start()
+        p_copy().start()
 
     a_copy(0).start()
-    d_copy(0).start()
-    p_copy().start()
-    own_x.start()
+    pl.when(z == 0)(beside_z)
     for r in range(rhs):
         for i in range(2):
             z_copy(r, i).start()
+    own_x.start()
     own_a.start()
+
+    @pl.when(z == 0)
+    def _():
+        pl.semaphore_wait(ready, 2)
+        pl.semaphore_signal(ready, inc=1, device_id=device(1), device_id_type=MESH)
+
+    @pl.when(z == 1)
+    def _():
+        pl.semaphore_wait(ready, 1)
+        beside_z()
 
     own_x.wait()
     p_copy(True).wait_recv()
@@ -218,6 +242,7 @@
                 pltpu.VMEM((rhs, SIDE * rows, cols // SIDE), x.dtype),
                 *sems,
                 pltpu.SemaphoreType.DMA((2,)),
+                pltpu.SemaphoreType.REGULAR,
             ],
             compiler_params=pltpu.CompilerParams(collective_id=0, has_side_effects=True, vmem_limit_bytes=52 * 1024 * 1024),
         )(w, x)

time: 154 us -> 153 us (level)
  no operation moved by 1% of the time
where the time goes in v7:
time: 153 us
  Pallas kernels  150 us (98%)
  local copies, waits for them, and re-layouts  2.71 us (2%)
    pallas_call x1, Pallas kernels, local(): pl.pallas_call(kernel, out_shape=pltpu.VMEM(x.shape, x.dtype), in_specs=[...  150 us

profile of v7, /device:TPU:0, one launch (start us, length us, event | category | flops | bytes accessed | tf_op | source)
XLA Modules:
  0.0 153.1 jit_solution(2148683353381384913)
XLA Ops:
  0.0 150.4 %shard_map.28 = bf16[3,256,4096]{2,1,0:T(8,128)(2,1)S(1)} custom-call(bf16[256,1024]{1,0:T(8,128)(2,1)} %w_ref.1, bf16[3,256,4096]{2,1,0:T(8,128)(2,1)} %x_ref.1), custom_call_target="tpu_custom_call" | custom-call | tf_op jit(solution)/shard_map/pallas_call | solution.py:234
  150.4 2.7 %copy.4 = bf16[3,256,4096]{2,1,0:T(8,128)(2,1)} copy(bf16[3,256,4096]{2,1,0:T(8,128)(2,1)S(1)} %shard_map.28) | data formatting | bytes 12582912

commit v8 on v7

--- a/solution.py
+++ b/solution.py
@@ -12,7 +12,7 @@
 WIDE = 256
 
 
-def kernel(w_ref, x_ref, y_ref, a_buf, x_buf, y_buf, a_send, a_recv, z_send, z_recv, d_send, d_recv, f_send, f_recv,
+def kernel(w_ref, x_ref, y_ref, a_buf, x_buf, y_buf, a_send, a_recv, in_send, in_recv, d_send, d_recv, f_send, f_recv,
            p_send, p_recv, y_send, y_recv, q_send, q_recv, own_sem, ready):
     z, j, row = lax.axis_index("depth"), lax.axis_index("col"), lax.axis_index("row")
     x, c = row // 2, row % 2
@@ -21,7 +21,7 @@
     group = cols // SIDE
 
     def peer(k):
-        kx, kc, kz = k // 4 % 2, k // 2 % 2, k % 2
+        kz, kc, kx = k // 4 % 2, k // 2 % 2, k % 2
         return x + kx * (1 - 2 * x), c + kc * (1 - 2 * c), z + kz * (1 - 2 * z)
 
     def device(k):
@@ -29,8 +29,8 @@
         return (pz, j, px * 2 + pc)
 
     def in_side(k):
-        _, pc, pz = peer(k)
-        return pc * 2 + pz
+        px, pc, _ = peer(k)
+        return pc * 2 + px
 
     other_y = (z, 1 - j, row)
 
@@ -38,8 +38,8 @@
         return pltpu.make_async_remote_copy(src, dst, send, recv, device_id=to, device_id_type=MESH)
 
     def a_block(k, jj):
-        _, pc, pz = peer(k)
-        return a_buf.at[pc, pz, :, pl.ds(pl.multiple_of(jj * kcols, kcols), kcols)]
+        px, pc, _ = peer(k)
+        return a_buf.at[pc, px, :, pl.ds(pl.multiple_of(jj * kcols, kcols), kcols)]
 
     def rows_of(k):
         return pl.ds(pl.multiple_of(in_side(k) * rows, rows), rows)
@@ -68,12 +68,12 @@
     def x_copy(piece, k, send, recv, receive=False):
         return remote(x_ref.at[given(piece, k)], held(piece, k if receive else 0), send, recv, device(k))
 
-    def z_copy(r, i, receive=False):
-        return x_copy((r, 0, group), (1, 3)[i], z_send.at[r, i], z_recv.at[r, i], receive)
-
-    def along_x(piece, side, send, recv, receive):
+    def in_copy(r, i, receive=False):
+        return x_copy((r, 0, group), (1, 3)[i], in_send.at[r, i], in_recv.at[r, i], receive)
+
+    def onward(piece, side, send, recv, receive):
         r, at, width = piece
-        src, here = (x_buf.at[r, px, :, side, :, pl.ds(at, width)] for px in (x, 1 - x))
+        src, here = (x_buf.at[r, side, :, pz, :, pl.ds(at, width)] for pz in (z, 1 - z))
         return remote(src, here if receive else src, send, recv, device(4))
 
     ahead = (pl.ds(0, SPLIT), 0, group)
@@ -81,12 +81,12 @@
     def d_copy(n, receive=False):
         if n == 0:
             return x_copy(ahead, 4, d_send.at[n], d_recv.at[n], receive)
-        src, here = (x_buf.at[ahead[0], px, 1 - c, z] for px in (x, 1 - x))
+        src, here = (x_buf.at[ahead[0], x, 1 - c, pz] for pz in (z, 1 - z))
         return remote(src, here if receive else src, d_send.at[n], d_recv.at[n], device(4))
 
     def f_copy(n, receive=False):
-        side = 1 - z if PIECES[n][0] < SPLIT else slice(None)
-        return along_x(PIECES[n], side, f_send.at[n], f_recv.at[n], receive)
+        side = 1 - x if PIECES[n][0] < SPLIT else slice(None)
+        return onward(PIECES[n], side, f_send.at[n], f_recv.at[n], receive)
 
     everything = (slice(None), 0, group)
 
@@ -108,13 +108,13 @@
 
     def product(k, r, at):
         xs = x_buf[r, :, :, :, :, pl.ds(at, WIDE)].reshape(-1, WIDE)
-        return jnp.dot(a_buf[peer(k)[1], peer(k)[2]], xs, preferred_element_type=jnp.float32).astype(y_buf.dtype)
+        return jnp.dot(a_buf[peer(k)[1], peer(k)[0]], xs, preferred_element_type=jnp.float32).astype(y_buf.dtype)
 
     def forward(n):
         r, at, _ = PIECES[n]
         if at == 0:
             for i in range(2):
-                z_copy(r, i, True).wait_recv()
+                in_copy(r, i, True).wait_recv()
         f_copy(n).start()
 
     def multiply(n):
@@ -154,7 +154,7 @@
     for k in (1, 3):
         pl.semaphore_signal(barrier, inc=1, device_id=device(k), device_id_type=MESH)
 
-    @pl.when(z == 0)
+    @pl.when(x == 0)
     def _():
         for to in (device(2), device(4), other_y):
             pl.semaphore_signal(barrier, inc=1, device_id=to, device_id_type=MESH)
@@ -162,31 +162,31 @@
         for to in (device(4), other_y):
             pl.semaphore_signal(ready, inc=1, device_id=to, device_id_type=MESH)
 
-    @pl.when(z == 1)
+    @pl.when(x == 1)
     def _():
         pl.semaphore_wait(barrier, 2)
 
-    def beside_z():
+    def other_links():
         d_copy(0).start()
         p_copy().start()
 
     a_copy(0).start()
-    pl.when(z == 0)(beside_z)
+    pl.when(x == 0)(other_links)
     for r in range(rhs):
         for i in range(2):
-            z_copy(r, i).start()
+            in_copy(r, i).start()
     own_x.start()
     own_a.start()
 
-    @pl.when(z == 0)
+    @pl.when(x == 0)
     def _():
         pl.semaphore_wait(ready, 2)
         pl.semaphore_signal(ready, inc=1, device_id=device(1), device_id_type=MESH)
 
-    @pl.when(z == 1)
+    @pl.when(x == 1)
     def _():
         pl.semaphore_wait(ready, 1)
-        beside_z()
+        other_links()
 
     own_x.wait()
     p_copy(True).wait_recv()
@@ -215,7 +215,7 @@
         d_copy(n).wait_send()
     for r in range(rhs):
         for i in range(2):
-            z_copy(r, i).wait_send()
+            in_copy(r, i).wait_send()
     q_copy().wait_send()
     q_copy(True).wait_recv()
     for n in range(len(PIECES)):

time: 153 us -> 153 us (level)
  no operation moved by 1% of the time
where the time goes in v8:
time: 153 us
  Pallas kernels  150 us (98%)
  local copies, waits for them, and re-layouts  2.71 us (2%)
    pallas_call x1, Pallas kernels, local(): pl.pallas_call(kernel, out_shape=pltpu.VMEM(x.shape, x.dtype), in_specs=[...  150 us

profile of v8, /device:TPU:0, one launch (start us, length us, event | category | flops | bytes accessed | tf_op | source)
XLA Modules:
  0.0 153.0 jit_solution(1055934408694722838)
XLA Ops:
  0.0 150.3 %shard_map.28 = bf16[3,256,4096]{2,1,0:T(8,128)(2,1)S(1)} custom-call(bf16[256,1024]{1,0:T(8,128)(2,1)} %w_ref.1, bf16[3,256,4096]{2,1,0:T(8,128)(2,1)} %x_ref.1), custom_call_target="tpu_custom_call" | custom-call | tf_op jit(solution)/shard_map/pallas_call | solution.py:234
  150.3 2.7 %copy.4 = bf16[3,256,4096]{2,1,0:T(8,128)(2,1)} copy(bf16[3,256,4096]{2,1,0:T(8,128)(2,1)S(1)} %shard_map.28) | data formatting | bytes 12582912

commit v9 on v8

--- a/solution.py
+++ b/solution.py
@@ -1,3 +1,5 @@
+import functools
+
 import jax
 import jax.numpy as jnp
 from jax import lax
@@ -10,10 +12,11 @@
 PIECES = ((0, 0, 1024), (1, 0, 1024), (2, 0, 512), (2, 512, 256), (2, 768, 256))
 SPLIT = 2
 WIDE = 256
+MOVED = 16
 
 
 def kernel(w_ref, x_ref, y_ref, a_buf, x_buf, y_buf, a_send, a_recv, in_send, in_recv, d_send, d_recv, f_send, f_recv,
-           p_send, p_recv, y_send, y_recv, q_send, q_recv, own_sem, ready):
+           p_send, p_recv, y_send, y_recv, q_send, q_recv, own_sem, ready, e_buf, e_send, e_recv):
     z, j, row = lax.axis_index("depth"), lax.axis_index("col"), lax.axis_index("row")
     x, c = row // 2, row % 2
     rhs, rows, cols = x_ref.shape
@@ -56,6 +59,31 @@
             src, to = there, device(2)
         return remote(src, here if receive else there, a_send.at[n], a_recv.at[n], to)
 
+    def a_over_x(op):
+        few = (j == 0) & (c == 0)
+
+        @pl.when(few)
+        def _():
+            rest = pl.ds(MOVED, rows - MOVED)
+            src, there, here = w_ref.at[rest, :], a_block(0, j).at[rest, :], a_block(1, j).at[rest, :]
+            op(lambda receive=False: remote(src, here if receive else there, a_send.at[0], a_recv.at[0], device(1)))
+
+        @pl.when(jnp.logical_not(few))
+        def _():
+            op(lambda receive=False: a_copy(0, receive))
+
+    def e_copy(n, receive=False):
+        if n == 0:
+            src, there, to = w_ref.at[pl.ds(0, MOVED), :], e_buf.at[0], other_y
+        elif n == 1:
+            src, there, to = e_buf.at[0], e_buf.at[1], device(1)
+        else:
+            src, there, to = e_buf.at[1], a_block(1, 0).at[pl.ds(0, MOVED), :], other_y
+        return remote(src, there, e_send.at[n], e_recv.at[n], to)
+
+    def when_moved(plane, body):
+        pl.when((j == plane) & (c == 0))(body)
+
     def given(piece, k):
         r, at, width = piece
         return (r, slice(None), pl.ds(pl.multiple_of(in_side(k) * group + at, WIDE), width))
@@ -170,29 +198,43 @@
         d_copy(0).start()
         p_copy().start()
 
-    a_copy(0).start()
+    a_over_x(lambda copy: copy().start())
     pl.when(x == 0)(other_links)
+    own_x.start()
+    own_a.start()
+
+    @pl.when(x == 0)
+    def _():
+        pl.semaphore_wait(ready, 2)
+        pl.semaphore_signal(ready, inc=1, device_id=device(1), device_id_type=MESH)
+
+    @pl.when(x == 1)
+    def _():
+        pl.semaphore_wait(ready, 1)
+        other_links()
+
+    when_moved(0, lambda: e_copy(0).start())
+
+    @functools.partial(when_moved, 1)
+    def _():
+        e_copy(0, True).wait_recv()
+        e_copy(1).start()
+
     for r in range(rhs):
         for i in range(2):
             in_copy(r, i).start()
-    own_x.start()
-    own_a.start()
-
-    @pl.when(x == 0)
-    def _():
-        pl.semaphore_wait(ready, 2)
-        pl.semaphore_signal(ready, inc=1, device_id=device(1), device_id_type=MESH)
-
-    @pl.when(x == 1)
-    def _():
-        pl.semaphore_wait(ready, 1)
-        other_links()
-
     own_x.wait()
     p_copy(True).wait_recv()
     d_copy(1).start()
     own_a.wait()
-    a_copy(0, True).wait_recv()
+    a_over_x(lambda copy: copy(True).wait_recv())
+
+    @functools.partial(when_moved, 1)
+    def _():
+        e_copy(1, True).wait_recv()
+        e_copy(2).start()
+
+    when_moved(0, lambda: e_copy(2, True).wait_recv())
     a_copy(1).start()
     a_copy(1, True).wait_recv()
     a_copy(2).start()
@@ -208,7 +250,15 @@
         multiply(n)
 
     q_copy().start()
-    for n in range(3):
+    a_over_x(lambda copy: copy().wait_send())
+    when_moved(0, lambda: e_copy(0).wait_send())
+
+    @functools.partial(when_moved, 1)
+    def _():
+        e_copy(1).wait_send()
+        e_copy(2).wait_send()
+
+    for n in range(1, 3):
         a_copy(n).wait_send()
     p_copy().wait_send()
     for n in range(2):
@@ -243,6 +293,9 @@
                 *sems,
                 pltpu.SemaphoreType.DMA((2,)),
                 pltpu.SemaphoreType.REGULAR,
+                pltpu.VMEM((2, MOVED, w.shape[1]), w.dtype),
+                pltpu.SemaphoreType.DMA((3,)),
+                pltpu.SemaphoreType.DMA((3,)),
             ],
             compiler_params=pltpu.CompilerParams(collective_id=0, has_side_effects=True, vmem_limit_bytes=52 * 1024 * 1024),
         )(w, x)

time: 153 us -> 153 us (level)
  no operation moved by 1% of the time
where the time goes in v9:
time: 153 us
  Pallas kernels  150 us (98%)
  local copies, waits for them, and re-layouts  2.71 us (2%)
    pallas_call x1, Pallas kernels, local(): pl.pallas_call(kernel, out_shape=pltpu.VMEM(x.shape, x.dtype), in_specs=[...  150 us

profile of v9, /device:TPU:0, one launch (start us, length us, event | category | flops | bytes accessed | tf_op | source)
XLA Modules:
  0.0 152.7 jit_solution(3298982661162975550)
XLA Ops:
  0.0 150.0 %shard_map.28 = bf16[3,256,4096]{2,1,0:T(8,128)(2,1)S(1)} custom-call(bf16[256,1024]{1,0:T(8,128)(2,1)} %w_ref.1, bf16[3,256,4096]{2,1,0:T(8,128)(2,1)} %x_ref.1), custom_call_target="tpu_custom_call" | custom-call | tf_op jit(solution)/shard_map/pallas_call | solution.py:284
  150.0 2.7 %copy.4 = bf16[3,256,4096]{2,1,0:T(8,128)(2,1)} copy(bf16[3,256,4096]{2,1,0:T(8,128)(2,1)S(1)} %shard_map.28) | data formatting | bytes 12582912

commit v10 on v9

--- a/solution.py
+++ b/solution.py
@@ -179,20 +179,20 @@
         lax.fori_loop(0, parts, own, 0)
 
     barrier = pltpu.get_barrier_semaphore()
-    for k in (1, 3):
-        pl.semaphore_signal(barrier, inc=1, device_id=device(k), device_id_type=MESH)
+    pl.semaphore_signal(barrier, inc=1, device_id=device(1), device_id_type=MESH)
+    beside = (device(4), other_y, device(2))
 
     @pl.when(x == 0)
     def _():
-        for to in (device(2), device(4), other_y):
+        for to in beside:
             pl.semaphore_signal(barrier, inc=1, device_id=to, device_id_type=MESH)
-        pl.semaphore_wait(barrier, 5)
-        for to in (device(4), other_y):
+        pl.semaphore_wait(barrier, 4)
+        for to in beside:
             pl.semaphore_signal(ready, inc=1, device_id=to, device_id_type=MESH)
 
     @pl.when(x == 1)
     def _():
-        pl.semaphore_wait(barrier, 2)
+        pl.semaphore_wait(barrier, 1)
 
     def other_links():
         d_copy(0).start()
@@ -205,7 +205,7 @@
 
     @pl.when(x == 0)
     def _():
-        pl.semaphore_wait(ready, 2)
+        pl.semaphore_wait(ready, 3)
         pl.semaphore_signal(ready, inc=1, device_id=device(1), device_id_type=MESH)
 
     @pl.when(x == 1)

time: 153 us -> 152 us (level)
  no operation moved by 1% of the time
where the time goes in v10:
time: 152 us
  Pallas kernels  150 us (99%)
  local copies, waits for them, and re-layouts  2.71 us (2%)
    pallas_call x1, Pallas kernels, local(): pl.pallas_call(kernel, out_shape=pltpu.VMEM(x.shape, x.dtype), in_specs=[...  150 us

profile of v10, /device:TPU:0, one launch (start us, length us, event | category | flops | bytes accessed | tf_op | source)
XLA Modules:
  0.0 152.2 jit_solution(17640916959373982537)
XLA Ops:
  0.0 149.5 %shard_map.28 = bf16[3,256,4096]{2,1,0:T(8,128)(2,1)S(1)} custom-call(bf16[256,1024]{1,0:T(8,128)(2,1)} %w_ref.1, bf16[3,256,4096]{2,1,0:T(8,128)(2,1)} %x_ref.1), custom_call_target="tpu_custom_call" | custom-call | tf_op jit(solution)/shard_map/pallas_call | solution.py:284
  149.5 2.7 %copy.4 = bf16[3,256,4096]{2,1,0:T(8,128)(2,1)} copy(bf16[3,256,4096]{2,1,0:T(8,128)(2,1)S(1)} %shard_map.28) | data formatting | bytes 12582912

commit v11 on v10

--- a/solution.py
+++ b/solution.py
@@ -181,6 +181,8 @@
     barrier = pltpu.get_barrier_semaphore()
     pl.semaphore_signal(barrier, inc=1, device_id=device(1), device_id_type=MESH)
     beside = (device(4), other_y, device(2))
+    own_x.start()
+    own_a.start()
 
     @pl.when(x == 0)
     def _():
@@ -200,8 +202,6 @@
 
     a_over_x(lambda copy: copy().start())
     pl.when(x == 0)(other_links)
-    own_x.start()
-    own_a.start()
 
     @pl.when(x == 0)
     def _():

time: 152 us -> 152 us (level)
  no operation moved by 1% of the time
where the time goes in v11:
time: 152 us
  Pallas kernels  150 us (99%)
  local copies, waits for them, and re-layouts  2.71 us (2%)
    pallas_call x1, Pallas kernels, local(): pl.pallas_call(kernel, out_shape=pltpu.VMEM(x.shape, x.dtype), in_specs=[...  150 us

profile of v11, /device:TPU:0, one launch (start us, length us, event | category | flops | bytes accessed | tf_op | source)
XLA Modules:
  0.0 152.2 jit_solution(215236161800979348)
XLA Ops:
  0.0 149.5 %shard_map.28 = bf16[3,256,4096]{2,1,0:T(8,128)(2,1)S(1)} custom-call(bf16[256,1024]{1,0:T(8,128)(2,1)} %w_ref.1, bf16[3,256,4096]{2,1,0:T(8,128)(2,1)} %x_ref.1), custom_call_target="tpu_custom_call" | custom-call | tf_op jit(solution)/shard_map/pallas_call | solution.py:284
  149.5 2.7 %copy.4 = bf16[3,256,4096]{2,1,0:T(8,128)(2,1)} copy(bf16[3,256,4096]{2,1,0:T(8,128)(2,1)S(1)} %shard_map.28) | data formatting | bytes 12582912

commit v12 on v11

--- a/solution.py
+++ b/solution.py
@@ -16,7 +16,7 @@
 
 
 def kernel(w_ref, x_ref, y_ref, a_buf, x_buf, y_buf, a_send, a_recv, in_send, in_recv, d_send, d_recv, f_send, f_recv,
-           p_send, p_recv, y_send, y_recv, q_send, q_recv, own_sem, ready, e_buf, e_send, e_recv):
+           p_send, p_recv, y_send, y_recv, q_send, q_recv, own_sem, ready, e_buf, g_buf, e_send, e_recv):
     z, j, row = lax.axis_index("depth"), lax.axis_index("col"), lax.axis_index("row")
     x, c = row // 2, row % 2
     rhs, rows, cols = x_ref.shape
@@ -59,18 +59,49 @@
             src, to = there, device(2)
         return remote(src, here if receive else there, a_send.at[n], a_recv.at[n], to)
 
-    def a_over_x(op):
-        few = (j == 0) & (c == 0)
-
-        @pl.when(few)
+    half = kcols // 2
+    last = pl.ds(rows - MOVED, MOVED)
+
+    def a_over_x(side, op):
+        low = (j == 0) & (z == 0) & (c == 0)
+        high = (z == 0) & (x == side) & (c == 0)
+
+        def some(cut_low, cut_high):
+            at = pl.ds(MOVED * cut_low, rows - MOVED * (cut_low + cut_high))
+
+            def copy(receive=False):
+                dst = a_block(1 if receive else 0, j).at[at, :]
+                return remote(w_ref.at[at, :], dst, a_send.at[0], a_recv.at[0], device(1))
+
+            has_low = low if cut_low else jnp.logical_not(low)
+            has_high = high if cut_high else jnp.logical_not(high)
+            pl.when(has_low & has_high)(lambda: op(copy))
+
+        for cut_low in range(2):
+            for cut_high in range(2):
+                some(cut_low, cut_high)
+
+        @pl.when(high)
         def _():
-            rest = pl.ds(MOVED, rows - MOVED)
-            src, there, here = w_ref.at[rest, :], a_block(0, j).at[rest, :], a_block(1, j).at[rest, :]
-            op(lambda receive=False: remote(src, here if receive else there, a_send.at[0], a_recv.at[0], device(1)))
-
-        @pl.when(jnp.logical_not(few))
-        def _():
-            op(lambda receive=False: a_copy(0, receive))
+            at = (last, pl.ds(half, half))
+
+            def copy(receive=False):
+                dst = a_block(1 if receive else 0, j).at[at]
+                return remote(w_ref.at[at], dst, e_send.at[3], e_recv.at[3], device(1))
+
+            op(copy)
+
+    def g_copy(n):
+        at = (last, pl.ds(0, half))
+        src, there, to = (
+            (w_ref.at[at], g_buf.at[0], device(4)),
+            (g_buf.at[0], g_buf.at[1], device(1)),
+            (g_buf.at[1], a_block(1, j).at[at], device(4)),
+        )[n]
+        return remote(src, there, e_send.at[4 + n], e_recv.at[4 + n], to)
+
+    def when_at(px, pz, body):
+        pl.when((x == px) & (z == pz) & (c == 0))(body)
 
     def e_copy(n, receive=False):
         if n == 0:
@@ -82,7 +113,7 @@
         return remote(src, there, e_send.at[n], e_recv.at[n], to)
 
     def when_moved(plane, body):
-        pl.when((j == plane) & (c == 0))(body)
+        pl.when((j == plane) & (z == 0) & (c == 0))(body)
 
     def given(piece, k):
         r, at, width = piece
@@ -197,10 +228,11 @@
         pl.semaphore_wait(barrier, 1)
 
     def other_links():
+        when_at(0, 0, lambda: g_copy(0).start())
         d_copy(0).start()
         p_copy().start()
 
-    a_over_x(lambda copy: copy().start())
+    a_over_x(0, lambda copy: copy().start())
     pl.when(x == 0)(other_links)
 
     @pl.when(x == 0)
@@ -219,15 +251,26 @@
     def _():
         e_copy(0, True).wait_recv()
         e_copy(1).start()
+
+    @functools.partial(when_at, 0, 1)
+    def _():
+        g_copy(0).wait_recv()
+        g_copy(1).start()
 
     for r in range(rhs):
         for i in range(2):
             in_copy(r, i).start()
     own_x.wait()
     p_copy(True).wait_recv()
+
+    @functools.partial(when_at, 1, 1)
+    def _():
+        g_copy(1).wait_recv()
+        g_copy(2).start()
+
     d_copy(1).start()
     own_a.wait()
-    a_over_x(lambda copy: copy(True).wait_recv())
+    a_over_x(1, lambda copy: copy(True).wait_recv())
 
     @functools.partial(when_moved, 1)
     def _():
@@ -235,11 +278,12 @@
         e_copy(2).start()
 
     when_moved(0, lambda: e_copy(2, True).wait_recv())
+    when_at(1, 0, lambda: g_copy(2).wait_recv())
     a_copy(1).start()
+    forward(0)
     a_copy(1, True).wait_recv()
     a_copy(2).start()
     a_copy(2, True).wait_recv()
-    forward(0)
     forward(1)
     multiply(0)
     forward(2)
@@ -250,7 +294,10 @@
         multiply(n)
 
     q_copy().start()
-    a_over_x(lambda copy: copy().wait_send())
+    a_over_x(0, lambda copy: copy().wait_send())
+    when_at(0, 0, lambda: g_copy(0).wait_send())
+    when_at(0, 1, lambda: g_copy(1).wait_send())
+    when_at(1, 1, lambda: g_copy(2).wait_send())
     when_moved(0, lambda: e_copy(0).wait_send())
 
     @functools.partial(when_moved, 1)
@@ -294,8 +341,9 @@
                 pltpu.SemaphoreType.DMA((2,)),
                 pltpu.SemaphoreType.REGULAR,
                 pltpu.VMEM((2, MOVED, w.shape[1]), w.dtype),
-                pltpu.SemaphoreType.DMA((3,)),
-                pltpu.SemaphoreType.DMA((3,)),
+                pltpu.VMEM((2, MOVED, w.shape[1] // 2), w.dtype),
+                pltpu.SemaphoreType.DMA((7,)),
+                pltpu.SemaphoreType.DMA((7,)),
             ],
             compiler_params=pltpu.CompilerParams(collective_id=0, has_side_effects=True, vmem_limit_bytes=52 * 1024 * 1024),
         )(w, x)

time: 152 us -> 152 us (level)
  no operation moved by 1% of the time
where the time goes in v12:
time: 152 us
  Pallas kernels  149 us (98%)
  local copies, waits for them, and re-layouts  2.71 us (2%)
    pallas_call x1, Pallas kernels, local(): pl.pallas_call(kernel, out_shape=pltpu.VMEM(x.shape, x.dtype), in_specs=[...  149 us

profile of v12, /device:TPU:0, one launch (start us, length us, event | category | flops | bytes accessed | tf_op | source)
XLA Modules:
  0.0 152.1 jit_solution(11278084684599396938)
XLA Ops:
  0.0 149.4 %shard_map.28 = bf16[3,256,4096]{2,1,0:T(8,128)(2,1)S(1)} custom-call(bf16[256,1024]{1,0:T(8,128)(2,1)} %w_ref.1, bf16[3,256,4096]{2,1,0:T(8,128)(2,1)} %x_ref.1), custom_call_target="tpu_custom_call" | custom-call | tf_op jit(solution)/shard_map/pallas_call | solution.py:331
  149.4 2.7 %copy.4 = bf16[3,256,4096]{2,1,0:T(8,128)(2,1)} copy(bf16[3,256,4096]{2,1,0:T(8,128)(2,1)S(1)} %shard_map.28) | data formatting | bytes 12582912

commit v13 on v12

--- a/solution.py
+++ b/solution.py
@@ -59,15 +59,15 @@
             src, to = there, device(2)
         return remote(src, here if receive else there, a_send.at[n], a_recv.at[n], to)
 
-    half = kcols // 2
-    last = pl.ds(rows - MOVED, MOVED)
+    few = MOVED // 2
+    last = pl.ds(rows - few, few)
 
     def a_over_x(side, op):
         low = (j == 0) & (z == 0) & (c == 0)
         high = (z == 0) & (x == side) & (c == 0)
 
         def some(cut_low, cut_high):
-            at = pl.ds(MOVED * cut_low, rows - MOVED * (cut_low + cut_high))
+            at = pl.ds(MOVED * cut_low, rows - MOVED * cut_low - few * cut_high)
 
             def copy(receive=False):
                 dst = a_block(1 if receive else 0, j).at[at, :]
@@ -81,24 +81,14 @@
             for cut_high in range(2):
                 some(cut_low, cut_high)
 
-        @pl.when(high)
-        def _():
-            at = (last, pl.ds(half, half))
-
-            def copy(receive=False):
-                dst = a_block(1 if receive else 0, j).at[at]
-                return remote(w_ref.at[at], dst, e_send.at[3], e_recv.at[3], device(1))
-
-            op(copy)
-
     def g_copy(n):
-        at = (last, pl.ds(0, half))
+        at = (last, slice(None))
         src, there, to = (
             (w_ref.at[at], g_buf.at[0], device(4)),
             (g_buf.at[0], g_buf.at[1], device(1)),
             (g_buf.at[1], a_block(1, j).at[at], device(4)),
         )[n]
-        return remote(src, there, e_send.at[4 + n], e_recv.at[4 + n], to)
+        return remote(src, there, e_send.at[3 + n], e_recv.at[3 + n], to)
 
     def when_at(px, pz, body):
         pl.when((x == px) & (z == pz) & (c == 0))(body)
@@ -341,9 +331,9 @@
                 pltpu.SemaphoreType.DMA((2,)),
                 pltpu.SemaphoreType.REGULAR,
                 pltpu.VMEM((2, MOVED, w.shape[1]), w.dtype),
-                pltpu.VMEM((2, MOVED, w.shape[1] // 2), w.dtype),
-                pltpu.SemaphoreType.DMA((7,)),
-                pltpu.SemaphoreType.DMA((7,)),
+                pltpu.VMEM((2, MOVED // 2, w.shape[1]), w.dtype),
+                pltpu.SemaphoreType.DMA((6,)),
+                pltpu.SemaphoreType.DMA((6,)),
             ],
             compiler_params=pltpu.CompilerParams(collective_id=0, has_side_effects=True, vmem_limit_bytes=52 * 1024 * 1024),
         )(w, x)

time: 152 us -> 152 us (level)
  no operation moved by 1% of the time
where the time goes in v13:
time: 152 us
  Pallas kernels  149 us (98%)
  local copies, waits for them, and re-layouts  2.71 us (2%)
    pallas_call x1, Pallas kernels, local(): pl.pallas_call(kernel, out_shape=pltpu.VMEM(x.shape, x.dtype), in_specs=[...  149 us

profile of v13, /device:TPU:0, one launch (start us, length us, event | category | flops | bytes accessed | tf_op | source)
XLA Modules:
  0.0 152.1 jit_solution(949368719559641661)
XLA Ops:
  0.0 149.4 %shard_map.28 = bf16[3,256,4096]{2,1,0:T(8,128)(2,1)S(1)} custom-call(bf16[256,1024]{1,0:T(8,128)(2,1)} %w_ref.1, bf16[3,256,4096]{2,1,0:T(8,128)(2,1)} %x_ref.1), custom_call_target="tpu_custom_call" | custom-call | tf_op jit(solution)/shard_map/pallas_call | solution.py:321
  149.4 2.7 %copy.4 = bf16[3,256,4096]{2,1,0:T(8,128)(2,1)} copy(bf16[3,256,4096]{2,1,0:T(8,128)(2,1)S(1)} %shard_map.28) | data formatting | bytes 12582912

commit v14 on v13

--- a/solution.py
+++ b/solution.py
@@ -62,9 +62,9 @@
     few = MOVED // 2
     last = pl.ds(rows - few, few)
 
-    def a_over_x(side, op):
+    def a_over_x(op):
         low = (j == 0) & (z == 0) & (c == 0)
-        high = (z == 0) & (x == side) & (c == 0)
+        high = (z == 0) & (c == 0)
 
         def some(cut_low, cut_high):
             at = pl.ds(MOVED * cut_low, rows - MOVED * cut_low - few * cut_high)
@@ -90,8 +90,8 @@
         )[n]
         return remote(src, there, e_send.at[3 + n], e_recv.at[3 + n], to)
 
-    def when_at(px, pz, body):
-        pl.when((x == px) & (z == pz) & (c == 0))(body)
+    def when_at(pz, body):
+        pl.when((z == pz) & (c == 0))(body)
 
     def e_copy(n, receive=False):
         if n == 0:
@@ -218,11 +218,11 @@
         pl.semaphore_wait(barrier, 1)
 
     def other_links():
-        when_at(0, 0, lambda: g_copy(0).start())
+        when_at(0, lambda: g_copy(0).start())
         d_copy(0).start()
         p_copy().start()
 
-    a_over_x(0, lambda copy: copy().start())
+    a_over_x(lambda copy: copy().start())
     pl.when(x == 0)(other_links)
 
     @pl.when(x == 0)
@@ -242,7 +242,7 @@
         e_copy(0, True).wait_recv()
         e_copy(1).start()
 
-    @functools.partial(when_at, 0, 1)
+    @functools.partial(when_at, 1)
     def _():
         g_copy(0).wait_recv()
         g_copy(1).start()
@@ -253,14 +253,14 @@
     own_x.wait()
     p_copy(True).wait_recv()
 
-    @functools.partial(when_at, 1, 1)
+    @functools.partial(when_at, 1)
     def _():
         g_copy(1).wait_recv()
         g_copy(2).start()
 
     d_copy(1).start()
     own_a.wait()
-    a_over_x(1, lambda copy: copy(True).wait_recv())
+    a_over_x(lambda copy: copy(True).wait_recv())
 
     @functools.partial(when_moved, 1)
     def _():
@@ -268,7 +268,7 @@
         e_copy(2).start()
 
     when_moved(0, lambda: e_copy(2, True).wait_recv())
-    when_at(1, 0, lambda: g_copy(2).wait_recv())
+    when_at(0, lambda: g_copy(2).wait_recv())
     a_copy(1).start()
     forward(0)
     a_copy(1, True).wait_recv()
@@ -284,10 +284,10 @@
         multiply(n)
 
     q_copy().start()
-    a_over_x(0, lambda copy: copy().wait_send())
-    when_at(0, 0, lambda: g_copy(0).wait_send())
-    when_at(0, 1, lambda: g_copy(1).wait_send())
-    when_at(1, 1, lambda: g_copy(2).wait_send())
+    a_over_x(lambda copy: copy().wait_send())
+    when_at(0, lambda: g_copy(0).wait_send())
+    when_at(1, lambda: g_copy(1).wait_send())
+    when_at(1, lambda: g_copy(2).wait_send())
     when_moved(0, lambda: e_copy(0).wait_send())
 
     @functools.partial(when_moved, 1)

time: 152 us -> 152 us (level)
  no operation moved by 1% of the time
where the time goes in v14:
time: 152 us
  Pallas kernels  149 us (98%)
  local copies, waits for them, and re-layouts  2.71 us (2%)
    pallas_call x1, Pallas kernels, local(): pl.pallas_call(kernel, out_shape=pltpu.VMEM(x.shape, x.dtype), in_specs=[...  149 us

profile of v14, /device:TPU:0, one launch (start us, length us, event | category | flops | bytes accessed | tf_op | source)
XLA Modules:
  0.0 152.1 jit_solution(6677818744121855066)
XLA Ops:
  0.0 149.4 %shard_map.28 = bf16[3,256,4096]{2,1,0:T(8,128)(2,1)S(1)} custom-call(bf16[256,1024]{1,0:T(8,128)(2,1)} %w_ref.1, bf16[3,256,4096]{2,1,0:T(8,128)(2,1)} %x_ref.1), custom_call_target="tpu_custom_call" | custom-call | tf_op jit(solution)/shard_map/pallas_call | solution.py:321
  149.4 2.7 %copy.4 = bf16[3,256,4096]{2,1,0:T(8,128)(2,1)} copy(bf16[3,256,4096]{2,1,0:T(8,128)(2,1)S(1)} %shard_map.28) | data formatting | bytes 12582912

commit v15 on v14

--- a/solution.py
+++ b/solution.py
@@ -63,7 +63,7 @@
     last = pl.ds(rows - few, few)
 
     def a_over_x(op):
-        low = (j == 0) & (z == 0) & (c == 0)
+        low = (j == 0) & (z == 0) & (c == 1)
         high = (z == 0) & (c == 0)
 
         def some(cut_low, cut_high):
@@ -103,7 +103,7 @@
         return remote(src, there, e_send.at[n], e_recv.at[n], to)
 
     def when_moved(plane, body):
-        pl.when((j == plane) & (z == 0) & (c == 0))(body)
+        pl.when((j == plane) & (z == 0) & (c == 1))(body)
 
     def given(piece, k):
         r, at, width = piece

time: 152 us -> 152 us (level)
  no operation moved by 1% of the time
where the time goes in v15:
time: 152 us
  Pallas kernels  149 us (98%)
  local copies, waits for them, and re-layouts  2.71 us (2%)
    pallas_call x1, Pallas kernels, local(): pl.pallas_call(kernel, out_shape=pltpu.VMEM(x.shape, x.dtype), in_specs=[...  149 us

profile of v15, /device:TPU:0, one launch (start us, length us, event | category | flops | bytes accessed | tf_op | source)
XLA Modules:
  0.0 152.1 jit_solution(13666698590609462263)
XLA Ops:
  0.0 149.4 %shard_map.28 = bf16[3,256,4096]{2,1,0:T(8,128)(2,1)S(1)} custom-call(bf16[256,1024]{1,0:T(8,128)(2,1)} %w_ref.1, bf16[3,256,4096]{2,1,0:T(8,128)(2,1)} %x_ref.1), custom_call_target="tpu_custom_call" | custom-call | tf_op jit(solution)/shard_map/pallas_call | solution.py:321
  149.4 2.7 %copy.4 = bf16[3,256,4096]{2,1,0:T(8,128)(2,1)} copy(bf16[3,256,4096]{2,1,0:T(8,128)(2,1)S(1)} %shard_map.28) | data formatting | bytes 12582912
